TPU v7x, 128 devices: a whole 4x4x4 slice. The times are simulated.
128 devices in a mesh: sp: 4 (over x), dp: 32 (over z, y, core).
Axes of the slice: x: 4, y: 4, z: 4, core: 2. Of those that a mesh axis runs over, the one named last changes fastest.
Arguments:
- hidden_in: bfloat16 [65536, 768], P(('dp', 'sp'))
- cu_seqlens: int32 [32, 9], P('dp')
- pos_ids: int32 [65536], P(('dp', 'sp'))
- w_qkv: bfloat16 [2, 768, 2304], replicated
- w_attn_out: bfloat16 [2, 768, 768], replicated
- w_mlp_in: bfloat16 [2, 768, 6144], replicated
- w_mlp_out: bfloat16 [2, 3072, 768], replicated
- ln_attn: float32 [2, 768], replicated
- ln_mlp: float32 [2, 768], replicated
- d_out: bfloat16 [65536, 768], P(('dp', 'sp'))
Outputs:
- output 1: bfloat16 [65536, 768], P(('dp', 'sp'))
- output 2: bfloat16 [65536, 768], P(('dp', 'sp'))
- output 3: float32 [2, 768, 2304], replicated
- output 4: float32 [2, 768, 768], replicated
- output 5: float32 [2, 768, 6144], replicated
- output 6: float32 [2, 3072, 768], replicated
- output 7: float32 [2, 768], replicated
- output 8: float32 [2, 768], replicated
All inputs are finite; a program needn't handle non-finite values.
Results may differ from a plain program's by a relative error of at most 0.02.
Values are sent between devices in bfloat16 or wider.
A program may use at most 1 GiB of HBM per device.

v0:
```python
import functools
import math
import jax
import jax.numpy as jnp
from jax import lax
from jax.sharding import PartitionSpec as P

HEAD_DIM = 64
WINDOW_HALF = 64
LN_EPS = 1e-5
NEG_BIG = -1e30
LAYER_KINDS = ((160000.0, False), (10000.0, True))


def layer_norm(in_rows, gain_row):
    rows32 = in_rows.astype(jnp.float32)
    centered = rows32 - jnp.mean(rows32, axis=-1, keepdims=True)
    var_row = jnp.mean(centered * centered, axis=-1, keepdims=True)
    return (centered * lax.rsqrt(var_row + LN_EPS) * gain_row).astype(jnp.bfloat16)


def rope_rows(qkv_rows, pos_ids, rope_base):
    half_dim = HEAD_DIM // 2
    inv_freq = rope_base ** (jnp.arange(half_dim).astype(jnp.float32) * (-2.0 / HEAD_DIM))
    angles = pos_ids.astype(jnp.float32)[:, None] * inv_freq[None, :]
    cos_tab = jnp.concatenate([jnp.cos(angles), jnp.cos(angles)], axis=-1)[:, None, None, :]
    sin_tab = jnp.concatenate([jnp.sin(angles), jnp.sin(angles)], axis=-1)[:, None, None, :]
    qk_rows = qkv_rows[:, :2].astype(jnp.float32)
    rotated = jnp.concatenate([-qk_rows[..., half_dim:], qk_rows[..., :half_dim]], axis=-1)
    turned = (qk_rows * cos_tab + rotated * sin_tab).astype(jnp.bfloat16)
    return jnp.concatenate([turned, qkv_rows[:, 2:]], axis=1)


def geglu(up_rows):
    ff_dim = up_rows.shape[-1] // 2
    gate_in = up_rows.astype(jnp.float32)
    return (jax.nn.gelu(gate_in[:, :ff_dim], approximate=False) * gate_in[:, ff_dim:]).astype(jnp.bfloat16)


def doc_ids_at(cu_row, token_idx, n_group):
    inside = jnp.sum((cu_row[None, 1:-1] <= token_idx[:, None]).astype(jnp.int32), axis=1)
    valid = (token_idx >= 0) & (token_idx < n_group)
    return jnp.where(valid, inside, -1)


def global_attention(query_rows, key_rows, val_rows, doc_ids):
    n_tok = query_rows.shape[0]
    q_block = math.gcd(n_tok, 256)
    score_scale = HEAD_DIM ** -0.5

    def one_block(blk_start):
        q_blk = lax.dynamic_slice_in_dim(query_rows, blk_start, q_block, 0)
        doc_blk = lax.dynamic_slice_in_dim(doc_ids, blk_start, q_block, 0)
        scores = jnp.einsum('qhd,khd->hqk', q_blk, key_rows, preferred_element_type=jnp.float32) * score_scale
        allowed = doc_blk[:, None] == doc_ids[None, :]
        scores = jnp.where(allowed[None], scores, NEG_BIG)
        prob_bf = jax.nn.softmax(scores, axis=-1).astype(jnp.bfloat16)
        return jnp.einsum('hqk,khd->qhd', prob_bf, val_rows, preferred_element_type=jnp.float32).astype(jnp.bfloat16)

    starts = jnp.arange(n_tok // q_block) * q_block
    return lax.map(jax.checkpoint(one_block), starts).reshape(query_rows.shape)


def banded_attention(query_rows, key_ext, val_ext, doc_q, doc_ext):
    n_tok, n_heads = query_rows.shape[0], query_rows.shape[1]
    tile_len = WINDOW_HALF
    n_blk = n_tok // tile_len

    def band_view(ext_rows):
        tile_rows = ext_rows.reshape((n_blk + 2, tile_len) + ext_rows.shape[1:])
        return jnp.concatenate([tile_rows[:-2], tile_rows[1:-1], tile_rows[2:]], axis=1)

    key_band = band_view(key_ext)
    val_band = band_view(val_ext)
    doc_band = band_view(doc_ext)
    q_tiles = query_rows.reshape(n_blk, tile_len, n_heads, HEAD_DIM)
    doc_tiles = doc_q.reshape(n_blk, tile_len)
    scores = jnp.einsum('bqhd,bkhd->bhqk', q_tiles, key_band, preferred_element_type=jnp.float32) * (HEAD_DIM ** -0.5)
    offset = jnp.arange(3 * tile_len)[None, :] - tile_len - jnp.arange(tile_len)[:, None]
    in_window = jnp.abs(offset) <= WINDOW_HALF
    allowed = (doc_tiles[:, :, None] == doc_band[:, None, :]) & in_window[None]
    scores = jnp.where(allowed[:, None], scores, NEG_BIG)
    prob_bf = jax.nn.softmax(scores, axis=-1).astype(jnp.bfloat16)
    attn_out = jnp.einsum('bhqk,bkhd->bqhd', prob_bf, val_band, preferred_element_type=jnp.float32).astype(jnp.bfloat16)
    return attn_out.reshape(query_rows.shape)


def head_attention(stacked, doc_ids, windowed):
    query_rows = stacked[:, 0]
    key_rows = stacked[:, 1]
    val_rows = stacked[:, 2]
    if not windowed:
        return global_attention(query_rows, key_rows, val_rows, doc_ids)
    pad_rows = jnp.zeros((WINDOW_HALF,) + key_rows.shape[1:], key_rows.dtype)
    pad_docs = jnp.full((WINDOW_HALF,), -1, jnp.int32)
    key_ext = jnp.concatenate([pad_rows, key_rows, pad_rows], axis=0)
    val_ext = jnp.concatenate([pad_rows, val_rows, pad_rows], axis=0)
    doc_ext = jnp.concatenate([pad_docs, doc_ids, pad_docs])
    return jax.checkpoint(banded_attention)(query_rows, key_ext, val_ext, doc_ids, doc_ext)


def head_exchange_attention(rot_qkv, doc_ids, windowed):
    head_qkv = lax.all_to_all(rot_qkv, 'sp', 2, 0, tiled=True)
    att_heads, attn_pull = jax.vjp(functools.partial(head_attention, doc_ids=doc_ids, windowed=windowed), head_qkv)
    att_tok = lax.all_to_all(att_heads, 'sp', 0, 1, tiled=True)

    def backward(d_att):
        d_heads = lax.all_to_all(d_att, 'sp', 1, 0, tiled=True)
        (d_head_qkv,) = attn_pull(d_heads)
        return lax.all_to_all(d_head_qkv, 'sp', 0, 2, tiled=True)

    return att_tok, backward


def weight_grad(left_rows, right_rows):
    return lax.dot_general(left_rows, right_rows, (((0,), (0,)), ((), ())), preferred_element_type=jnp.float32)


def input_grad(grad_rows, weight):
    return lax.dot_general(grad_rows, weight, (((1,), (1,)), ((), ())), preferred_element_type=jnp.float32).astype(jnp.bfloat16)


def layer_forward(x_rows, pos_ids, params, rope_base, attend):
    w_qkv, w_proj, w_up, w_down, g_attn, g_mlp = params
    n_tok, d_model = x_rows.shape
    n_heads = d_model // HEAD_DIM
    h_attn, ln1_pull = jax.vjp(layer_norm, x_rows, g_attn)
    qkv_rows = jnp.dot(h_attn, w_qkv, preferred_element_type=jnp.float32).astype(jnp.bfloat16)
    qkv_rows = qkv_rows.reshape(n_tok, 3, n_heads, HEAD_DIM)
    rot_qkv, rope_pull = jax.vjp(functools.partial(rope_rows, pos_ids=pos_ids, rope_base=rope_base), qkv_rows)
    att_rows, attn_back = attend(rot_qkv)
    att_flat = att_rows.reshape(n_tok, d_model)
    x_mid = (x_rows.astype(jnp.float32) + jnp.dot(att_flat, w_proj, preferred_element_type=jnp.float32)).astype(jnp.bfloat16)
    h_mlp, ln2_pull = jax.vjp(layer_norm, x_mid, g_mlp)
    up_rows = jnp.dot(h_mlp, w_up, preferred_element_type=jnp.float32).astype(jnp.bfloat16)
    act_rows, act_pull = jax.vjp(geglu, up_rows)
    y_rows = (x_mid.astype(jnp.float32) + jnp.dot(act_rows, w_down, preferred_element_type=jnp.float32)).astype(jnp.bfloat16)
    saved = (h_attn, ln1_pull, rope_pull, attn_back, att_flat, ln2_pull, h_mlp, act_pull, act_rows)
    return y_rows, saved


def layer_backward(d_y, saved, params):
    w_qkv, w_proj, w_up, w_down, g_attn, g_mlp = params
    h_attn, ln1_pull, rope_pull, attn_back, att_flat, ln2_pull, h_mlp, act_pull, act_rows = saved
    n_tok, d_model = d_y.shape
    n_heads = d_model // HEAD_DIM
    grad_down = weight_grad(act_rows, d_y)
    (d_up,) = act_pull(input_grad(d_y, w_down))
    grad_up = weight_grad(h_mlp, d_up)
    d_mid_ln, grad_gmlp = ln2_pull(input_grad(d_up, w_up))
    d_mid = d_y + d_mid_ln
    grad_proj = weight_grad(att_flat, d_mid)
    d_att = input_grad(d_mid, w_proj).reshape(n_tok, n_heads, HEAD_DIM)
    (d_qkv,) = rope_pull(attn_back(d_att))
    d_qkv_flat = d_qkv.reshape(n_tok, 3 * d_model)
    grad_qkv = weight_grad(h_attn, d_qkv_flat)
    d_x_ln, grad_gattn = ln1_pull(input_grad(d_qkv_flat, w_qkv))
    return d_mid + d_x_ln, (grad_qkv, grad_proj, grad_up, grad_down, grad_gattn, grad_gmlp)


def solution(mesh):
    sp_size = mesh.shape['sp']
    token_spec = P(('dp', 'sp'), None)

    def device_step(x_loc, cu_loc, pos_loc, w_qkv, w_proj, w_up, w_down, ln_attn, ln_mlp, d_out):
        n_group = x_loc.shape[0] * sp_size
        doc_ids = doc_ids_at(cu_loc[0], jnp.arange(n_group), n_group)
        all_params = (w_qkv, w_proj, w_up, w_down, ln_attn, ln_mlp)
        layer_params = [tuple(stack_w[layer_idx] for stack_w in all_params) for layer_idx in range(2)]
        hidden = x_loc
        saved_layers = []
        for layer_idx, (rope_base, windowed) in enumerate(LAYER_KINDS):
            attend = functools.partial(head_exchange_attention, doc_ids=doc_ids, windowed=windowed)
            hidden, saved = layer_forward(hidden, pos_loc, layer_params[layer_idx], rope_base, attend)
            saved_layers.append(saved)
        grad_rows = d_out
        layer_grads = [None, None]
        for layer_idx in (1, 0):
            grad_rows, layer_grads[layer_idx] = layer_backward(grad_rows, saved_layers[layer_idx], layer_params[layer_idx])
        stacked = tuple(jnp.stack([first_grad, second_grad]) for first_grad, second_grad in zip(layer_grads[0], layer_grads[1]))
        summed = lax.psum(stacked, ('sp', 'dp'))
        return (hidden, grad_rows) + tuple(summed)

    in_specs = (token_spec, P('dp', None), P(('dp', 'sp')), P(), P(), P(), P(), P(), P(), token_spec)
    out_specs = (token_spec, token_spec, P(), P(), P(), P(), P(), P())
    return jax.shard_map(device_step, mesh=mesh, in_specs=in_specs, out_specs=out_specs, check_vma=False)
```

profile of v0, /device:TPU:1, one launch (start us, length us, event | category | flops | bytes accessed | tf_op | source)
XLA Modules:
  0.0 1480.0 jit_solution(12463650043921125580)
XLA Ops:
  30.3 27.8 %all-to-all-done = bf16[512,3,12,64]{0,3,1,2:T(8,128)(2,1)S(1)} async-done(((bf16[512,3,12,64]{0,3,1,2:T(8,128)(2,1)}), bf16[512,3,12,64]{0,3,1,2:T(8,128)(2,1)S(1)}, u32[]{:S(2)}, u32[]{:S(2)}) %all-to-all-start) | async-done | bytes 2359328 | tf_op jit(solution)/shard_map/all_to_all | solution.py:103
  67.5 110.1 %while.30 = (s32[]{:T(128)}, bf16[8,256,3,64]{1,3,2,0:T(8,128)(2,1)}, s32[8]{0:T(128)S(1)}, s32[2048]{0:T(1024)S(1)}, s32[1,2048]{1,0:T(1,128)S(1)}, /*index=5*/...) while((s32[]{:T(128)}, ...), condition=%wide.region_6.7_spmd, body=%wide.region_3.6_spmd.sunk | while | flops 412665856 | bytes 15418543 | solution.py:61
  188.0 9.7 all-to-all-done.1
  205.6 7.8 fusion.77
  213.4 15.0 %multiply_convert_fusion.1 = (bf16[512,3072]{1,0:T(8,128)(2,1)S(1)}, f32[512,3072]{1,0:T(8,128)}) fusion(f32[512,6144]{1,0:T(8,128)S(1)} %fusion.77), kind=kLoop, calls=%fused_computation.126 | loop fusion | flops 103809024 | bytes 22020096 | tf_op jit(solution)/shard_map/jvp()/convert_element_type | solution.py:37
  252.3 24.1 %all-to-all-done.2 = bf16[512,3,12,64]{0,3,1,2:T(8,128)(2,1)S(1)} async-done(((bf16[512,3,12,64]{0,3,1,2:T(8,128)(2,1)}), bf16[512,3,12,64]{0,3,1,2:T(8,128)(2,1)S(1)}, u32[]{:S(2)}, u32[]{:S(2)}) %all-to-all-start.2) | async-done | bytes 2359328 | tf_op jit(solution)/shard_map/all_to_all | solution.py:103
  347.6 12.3 all_to_all.135
  367.8 7.8 fusion.83
  375.7 17.9 %convert_multiply_fusion.5 = (f32[512,3072]{1,0:T(8,128)}, f32[512,3072]{1,0:T(8,128)S(1)}, bf16[512,3072]{1,0:T(8,128)(2,1)}) fusion(f32[512,6144]{1,0:T(8,128)S(1)} %fusion.83, bf16[512,768]{1,0:T(8,128)(2,1)S(1)} %copy-done.54, bf16[2,3072,768]{2,1,0:T(8,128)(2,1)} %param.20), kind=kOutput, calls=%fused_computation.95 | convolution fusion | flops 2521300992 | bytes 27525120 | tf_op jit(solution)/shard_map/dot_general | solution.py:120
  393.6 7.4 multiply_add_fusion.1
  401.0 12.5 fusion.223
  526.9 6.8 copy.222
  533.7 7.1 reshape.446
  548.2 8.6 convolution_bitcast_fusion.4
  556.8 12.5 convolution_bitcast_fusion
  574.5 8.2 copy.224
  594.5 10.3 convert_multiply_fusion.2
  604.8 12.5 fusion.217
  617.4 14.5 convolution_bitcast_fusion.1
  646.5 14.8 pad_maximum_fusion.1
  670.7 189.1 %while.31 = (s32[]{:T(128)}, bf16[2048,3,64]{0,2,1:T(8,128)(2,1)S(1)}, bf16[2048,3,64]{0,2,1:T(8,128)(2,1)}, bf16[2048,3,64]{0,2,1:T(8,128)(2,1)}, s32[8]{0:T(12...) while((s32[]{:T(128)}, ...), condition=%wide.region_28.29_spmd.clone, body=%wide.region_24.28_spmd.clone.sunk | while | flops 1045941760 | bytes 77839648 | solution.py:61
  869.2 9.0 pad_add_fusion
  878.1 7.1 reshape.448
  894.3 27.8 %pad_maximum_fusion = f32[2,768,6144]{2,1,0:T(8,128)} fusion(f32[1,768,6144]{2,1,0:T(8,128)} %convolution_bitcast_fusion, f32[1,768,6144]{2,1,0:T(8,128)} %convolution_bitcast_fusion.1), kind=kLoop, calls=%fused_computation.65 | loop fusion | flops 9437184 | bytes 75497472 | tf_op jit(solution)/shard_map/stack | solution.py:180
  927.2 8.1 copy.232
  944.2 11.2 pad_maximum_fusion.2
  956.6 6.9 fusion.224
  968.9 75.8 %all-reduce.30 = (f32[2,768]{1,0:T(2,128)}, f32[2,768]{1,0:T(2,128)}) all-reduce(f32[2,768]{1,0:T(2,128)S(1)} %pad_maximum_fusion.13, f32[2,768]{1,0:T(2,128)S(1)} %pad_maximum_fusion.14), channel_id=1, replica_groups=mesh['sp'=4,'dp'=32] {'sp','dp'}, use_global_device_ids=true, to_apply=%region_37.38 | all-reduce | flops 3072 | bytes 24576 | tf_op jit(solution)/shard_map/psum | solution.py:181
  1046.3 372.6 %all-reduce.34.cloned.1.call-done = (f32[2,768,2304]{2,1,0:T(8,128)}, f32[2,768,768]{2,1,0:T(8,128)}, f32[2,768,6144]{2,1,0:T(8,128)}, f32[2,3072,768]{2,1,0:T(8,128)}) async-done(((f32[2,768,2304]{2,1,0:T(8,128)}, f32[2,768,768]{2,1,0:T(8,128)}, f32[2,768,6144]{2,1,0:T(8,128)}, f32[2,3072,768]{2,1,0:T(8,128)}), (f32[2,768,2304]{2,1,0:T(8,128)}, f32[2,768,768]{2,1,0:T(8,128)}, f32[2,768,6144]{2,1,0:T(8,128)}, ...) | async-done | bytes 75497488 | tf_op jit(solution)/shard_map/psum | solution.py:181
  1418.9 11.2 copy.278
  1435.1 31.0 %copy.280 = f32[2,768,6144]{2,1,0:T(8,128)} copy(f32[2,768,6144]{2,1,0:T(8,128)} %get-tuple-element.740) | data formatting | bytes 75497472
  1466.1 6.9 copy.281
  (576 shorter events, 626.9 us)
Async XLA Ops:
  11.4 223.6 %copy-start.66 = (f32[768]{0:T(1024)}, f32[768]{0:T(1024)S(1)}, u32[]{:S(2)}) copy-start(f32[768]{0:T(1024)S(1)} %get-tuple-element.400) | copy-start | bytes 9220
  24.8 33.3 %all-to-all-start = ((bf16[512,3,12,64]{0,3,1,2:T(8,128)(2,1)}), bf16[512,3,12,64]{0,3,1,2:T(8,128)(2,1)S(1)}, u32[]{:S(2)}, u32[]{:S(2)}) async-start(bf16[512,3,12,64]{0,3,1,2:T(8,128)(2,1)} %copy.185), calls=%async_computation | async-start | bytes 4718592 | tf_op jit(solution)/shard_map/all_to_all | solution.py:103
  30.2 35.9 %copy-start.62 = (s32[2048]{0:T(1024)}, s32[2048]{0:T(1024)S(1)}, u32[]{:S(2)}) copy-start(s32[2048]{0:T(1024)S(1)} %convert_reduce_fusion.4) | copy-start | bytes 24580
  177.6 256.7 %copy-start.51 = (s32[2048]{0:T(1024)}, s32[2048]{0:T(1024)S(1)}, u32[]{:S(2)}) copy-start(s32[2048]{0:T(1024)S(1)} %get-tuple-element.780) | copy-start | bytes 24580
  183.1 14.5 all-to-all-start.1
  187.9 14.9 %copy-start.3 = (bf16[512,768]{1,0:T(8,128)(2,1)S(1)}, bf16[512,768]{1,0:T(8,128)(2,1)}, u32[]{:S(2)}) copy-start(bf16[512,768]{1,0:T(8,128)(2,1)} %param.14) | copy-start | bytes 2359300
  187.9 17.7 %copy-start.56 = (f32[768]{0:T(1024)}, f32[768]{0:T(1024)S(1)}, u32[]{:S(2)}) copy-start(f32[768]{0:T(1024)S(1)} %get-tuple-element.399) | copy-start | bytes 9220
  187.9 56.3 %copy-start.47 = (f32[512,64]{0,1:T(8,128)}, f32[512,64]{0,1:T(8,128)S(1)}, u32[]{:S(2)}) copy-start(f32[512,64]{0,1:T(8,128)S(1)} %get-tuple-element.525) | copy-start | bytes 393220
  187.9 56.3 %copy-start.49 = (f32[512,64]{0,1:T(8,128)}, f32[512,64]{0,1:T(8,128)S(1)}, u32[]{:S(2)}) copy-start(f32[512,64]{0,1:T(8,128)S(1)} %get-tuple-element.526) | copy-start | bytes 393220
  205.1 23.2 %copy-start.8 = (bf16[512,768]{1,0:T(8,128)(2,1)}, bf16[512,768]{1,0:T(8,128)(2,1)S(1)}, u32[]{:S(2)}) copy-start(bf16[512,768]{1,0:T(8,128)(2,1)S(1)} %get-tuple-element.503) | copy-start | bytes 2359300
  213.4 15.0 %copy-start.5 = (f32[512,6144]{1,0:T(8,128)}, f32[512,6144]{1,0:T(8,128)S(1)}, u32[]{:S(2)}) copy-start(f32[512,6144]{1,0:T(8,128)S(1)} %fusion.77) | copy-start | bytes 37748740
  234.6 130.4 %copy-start.10 = (bf16[512,768]{1,0:T(8,128)(2,1)}, bf16[512,768]{1,0:T(8,128)(2,1)S(1)}, u32[]{:S(2)}) copy-start(bf16[512,768]{1,0:T(8,128)(2,1)S(1)} %get-tuple-element.505) | copy-start | bytes 2359300
  246.7 29.8 %all-to-all-start.2 = ((bf16[512,3,12,64]{0,3,1,2:T(8,128)(2,1)}), bf16[512,3,12,64]{0,3,1,2:T(8,128)(2,1)S(1)}, u32[]{:S(2)}, u32[]{:S(2)}) async-start(bf16[512,3,12,64]{0,3,1,2:T(8,128)(2,1)} %copy.193), calls=%async_computation.2 | async-start | bytes 4718592 | tf_op jit(solution)/shard_map/all_to_all | solution.py:103
  367.4 189.4 %copy-start.6 = (bf16[512,768]{1,0:T(8,128)(2,1)}, bf16[512,768]{1,0:T(8,128)(2,1)S(1)}, u32[]{:S(2)}) copy-start(bf16[512,768]{1,0:T(8,128)(2,1)S(1)} %get-tuple-element.509) | copy-start | bytes 2359300
  419.7 12.4 all-to-all-start.4
  540.8 28.5 %all-to-all-start.5 = ((bf16[4,2,147456]{2,1,0:T(2,128)(2,1)}), bf16[4,2,147456]{2,1,0:T(2,128)(2,1)S(1)}, u32[]{:S(2)}, u32[]{:S(2)}) async-start(bf16[4,2,147456]{2,1,0:T(2,128)(2,1)} %reshape.446), calls=%async_computation.5 | async-start | bytes 4718592 | tf_op jit(solution)/shard_map/all_to_all | solution.py:110
  544.5 12.4 slice-start
  604.8 12.5 copy-start.61
  617.3 19.7 %copy-start.31 = (bf16[512,768]{1,0:T(8,128)(2,1)}, bf16[512,768]{1,0:T(8,128)(2,1)S(1)}, u32[]{:S(2)}) copy-start(bf16[512,768]{1,0:T(8,128)(2,1)S(1)} %get-tuple-element.520) | copy-start | bytes 2359300
  617.3 14.5 copy-start.32
  617.3 14.5 copy-start.36
  640.3 20.9 %copy-start.16 = (bf16[512,768]{1,0:T(8,128)(2,1)}, bf16[512,768]{1,0:T(8,128)(2,1)S(1)}, u32[]{:S(2)}) copy-start(bf16[512,768]{1,0:T(8,128)(2,1)S(1)} %fusion.263) | copy-start | bytes 2359300
  642.3 26.4 %all-to-all-start.6 = ((bf16[512,12,64]{0,2,1:T(8,128)(2,1)}), bf16[512,12,64]{0,2,1:T(8,128)(2,1)S(1)}, u32[]{:S(2)}, u32[]{:S(2)}) async-start(bf16[512,12,64]{0,2,1:T(8,128)(2,1)} %bitcast.52), calls=%async_computation.6 | async-start | bytes 1572864 | tf_op jit(solution)/shard_map/all_to_all | solution.py:108
  646.5 14.8 copy-start.34
  885.2 36.9 %all-to-all-start.7 = ((bf16[4,2,147456]{2,1,0:T(2,128)(2,1)}), bf16[4,2,147456]{2,1,0:T(2,128)(2,1)S(1)}, u32[]{:S(2)}, u32[]{:S(2)}) async-start(bf16[4,2,147456]{2,1,0:T(2,128)(2,1)} %reshape.448), calls=%async_computation.7 | async-start | bytes 4718592 | tf_op jit(solution)/shard_map/all_to_all | solution.py:110
  889.4 529.5 %all-reduce.34.cloned.1.call-start = ((), (), s32[]{:S(2)}) async-start(), calls=%async_computation.8 | async-start | bytes 150994944 | tf_op jit(solution)/shard_map/psum | solution.py:181
  963.6 81.2 %copy-start.17 = (bf16[512,768]{1,0:T(8,128)(2,1)S(1)}, bf16[512,768]{1,0:T(8,128)(2,1)}, u32[]{:S(2)}) copy-start(bf16[512,768]{1,0:T(8,128)(2,1)} %copy-done.16) | copy-start | bytes 2359300
  1430.1 35.9 %slice-start.2 = ((s8[18874368]{0:T(1024)(128)(4,1)}), s8[2097152]{0:T(1024)(128)(4,1)S(1)}, s32[]{:S(2)}) async-start(s8[18874368]{0:T(1024)(128)(4,1)} %bitcast.314), calls=%async_computation.11 | async-start | bytes 4194304
  1435.1 31.0 %slice-start.3 = ((s8[18874368]{0:T(1024)(128)(4,1)}), s8[4194304]{0:T(1024)(128)(4,1)S(1)}, s32[]{:S(2)}) async-start(s8[18874368]{0:T(1024)(128)(4,1)} %bitcast.314), calls=%async_computation.12 | async-start | bytes 8388608
  1435.1 31.0 %slice-start.4 = ((s8[18874368]{0:T(1024)(128)(4,1)}), s8[4194304]{0:T(1024)(128)(4,1)S(1)}, s32[]{:S(2)}) async-start(s8[18874368]{0:T(1024)(128)(4,1)} %bitcast.314), calls=%async_computation.13 | async-start | bytes 8388608
  1435.1 31.0 %slice-start.5 = ((s8[18874368]{0:T(1024)(128)(4,1)}), s8[4194304]{0:T(1024)(128)(4,1)S(1)}, s32[]{:S(2)}) async-start(s8[18874368]{0:T(1024)(128)(4,1)} %bitcast.314), calls=%async_computation.14 | async-start | bytes 8388608
  1435.1 31.0 %slice-start.6 = ((s8[18874368]{0:T(1024)(128)(4,1)}), s8[4194304]{0:T(1024)(128)(4,1)S(1)}, s32[]{:S(2)}) async-start(s8[18874368]{0:T(1024)(128)(4,1)} %bitcast.314), calls=%async_computation.15 | async-start | bytes 8388608
  (92 other events, 413.9 us)
Sparse Core Ops, SparseCore 0:
  955.6 463.2 all-reduce.33
where the time goes:
time: 1490 us; the launch traced here: 1480 us
  waiting for transfers between devices  441 us (30%)
  matrix products  437 us (29%)
  local copies, waits for them, and re-layouts  300 us (20%)
  other arithmetic  136 us (9%)
  blocking collectives  88.1 us (6%)
  loops' own time  32 us (2%)
  starting transfers between devices  30.3 us (2%)
  between operations  16 us (1%)
    psum x1, waiting for transfers between devices, device_step(): summed = lax.psum(stacked, ('sp', 'dp'))  373 us
    sub x16, matrix products, one_block(): prob_bf = jax.nn.softmax(scores, axis=-1).astype(jnp.bfloat16)  99.3 us
    unnamed x213, local copies, waits for them, and re-layouts  97.2 us
    dot_general x24, matrix products, one_block(): jnp.einsum('hqk,khd->qhd', prob_bf, val_rows, preferred_element_type=jnp....  85.1 us
    psum x1, blocking collectives, device_step(): summed = lax.psum(stacked, ('sp', 'dp'))  75.8 us
    dot_general x8, matrix products, input_grad(): lax.dot_general(grad_rows, weight, (((1,), (1,)), ((), ())), preferred_el...  65.7 us
    another operation x6, other arithmetic, device_step(): jnp.stack([first_grad, second_grad])  58.7 us
    dot_general x8, matrix products, weight_grad(): lax.dot_general(left_rows, right_rows, (((0,), (0,)), ((), ())), preferre...  57.2 us
  transfers between devices with their start and end apart: 8, of which 5 were waited for; matrix products, arithmetic and copies ran while one was open for 7% of the time, Pallas kernels for 0%

commit v1 on v0

v1 whole, which is shorter than its diff:
```python
import functools
import math
import jax
import jax.numpy as jnp
from jax import lax
from jax.experimental import pallas as pl
from jax.experimental.pallas import tpu as pltpu
from jax.sharding import PartitionSpec as P

ZERO, ONE, TWO, THREE, FOUR = range(5)
SIX, TWELVE = 6, 12
HEAD = 64
HALF = 32
NHEAD = 12
DM = 768
FF = 3072
TOK = 512
GRP = 2048
WIN = 64
LANE = 128
EPS = 1e-5
NEG = -1e30
SCALE = 0.125
BASES = (160000.0, 10000.0)
F32 = jnp.float32
BF = jnp.bfloat16
QT = 256
FT = 512
NFT = FF // FT
QTILES = GRP // QT
MIB = 1024 * 1024
ALLTOK = (TOK, DM)
ANY = pl.BlockSpec(memory_space=pl.ANY)
DMA = pltpu.SemaphoreType.DMA
MESH = pl.DeviceIdType.MESH


def dot(a, b, ca, cb):
    return lax.dot_general(a, b, (((ca,), (cb,)), ((), ())), preferred_element_type=F32)


def mm(a, b):
    return dot(a, b, ONE, ZERO)


def mm_nt(a, b):
    return dot(a, b, ONE, ONE)


def mm_tn(a, b):
    return dot(a, b, ZERO, ZERO)


def call(body, grid, in_specs, out_specs, out_shape, scratch=(), prefetch=ZERO, flops=ZERO, nbytes=ZERO, name=None,
         cid=None, alias=None):
    extra = {} if cid is None else dict(collective_id=cid, has_side_effects=True)
    return pl.pallas_call(
        body,
        grid_spec=pltpu.PrefetchScalarGridSpec(
            num_scalar_prefetch=prefetch, grid=grid, in_specs=in_specs, out_specs=out_specs, scratch_shapes=scratch),
        out_shape=out_shape,
        input_output_aliases=alias or {},
        compiler_params=pltpu.CompilerParams(vmem_limit_bytes=60 * MIB, **extra),
        cost_estimate=pl.CostEstimate(flops=int(flops), bytes_accessed=int(nbytes), transcendentals=ZERO),
        name=name,
    )


def sds(shape, dtype):
    return jax.ShapeDtypeStruct(shape, dtype)


def spec(shape, *idx):
    idx = idx or (ZERO,) * len(shape)
    return pl.BlockSpec(shape, lambda *g: tuple(i(*g) if callable(i) else i for i in idx))


def step_of(s, *_):
    return s


def core_and_partner():
    dp = lax.axis_index('dp')
    core = lax.rem(dp, TWO)
    return core, {'dp': dp + ONE - TWO * core}


def meet_partner(partner):
    bar = pltpu.get_barrier_semaphore()
    pl.semaphore_signal(bar, inc=ONE, device_id=partner, device_id_type=MESH)
    pl.semaphore_wait(bar, ONE)


def to_partner(partner, src, dst, ssem, rsem):
    return pltpu.make_async_remote_copy(src_ref=src, dst_ref=dst, send_sem=ssem, recv_sem=rsem,
                                        device_id=partner, device_id_type=MESH)


def norm_parts(x_bf):
    rows = x_bf.astype(F32)
    cen = rows - jnp.mean(rows, axis=ONE, keepdims=True)
    var = jnp.mean(cen * cen, axis=ONE, keepdims=True)
    return cen, lax.rsqrt(var + EPS)


def norm_rows(x_bf, gain):
    cen, inv = norm_parts(x_bf)
    return (cen * inv * gain).astype(BF)


def norm_rows_grad(x_bf, gain, d_bf):
    cen, inv = norm_parts(x_bf)
    hat = cen * inv
    d_out = d_bf.astype(F32)
    g_gain = jnp.sum(d_out * hat, axis=ZERO, keepdims=True)
    d_hat = d_out * gain
    d_x = inv * (d_hat - jnp.mean(d_hat, axis=ONE, keepdims=True) - hat * jnp.mean(d_hat * hat, axis=ONE, keepdims=True))
    return d_x.astype(BF), g_gain


def add_bf(a, b):
    return (a.astype(F32) + b.astype(F32)).astype(BF)


PARTS = 9
ROPED = 6


def part_of(s, *_):
    return s // THREE


def slot_of(s, *_):
    return s % THREE


def head_rows(ref, head):
    return ref.at[head, ZERO, ZERO] if ref.shape[ZERO] == FOUR else ref.at[ZERO, ZERO, head]


def heads_spec(dest_major):
    if dest_major:
        return spec((FOUR, ONE, ONE, HEAD, TOK), ZERO, part_of, slot_of, ZERO, ZERO)
    return spec((ONE, ONE, FOUR, HEAD, TOK), part_of, slot_of, ZERO, ZERO, ZERO)


def weight_cols(layer, width, first=ZERO):
    return spec((None, DM, width), layer, ZERO, lambda s: first + s)


def qkv_fwd_body(x_ref, g_ref, w_ref, cos_ref, sin_ref, h_ref, out_ref, hr_ref, ssem, rsem):
    step = pl.program_id(ZERO)
    core, partner = core_and_partner()
    swap = to_partner(partner, h_ref, hr_ref, ssem, rsem)

    @pl.when(step == ZERO)
    def _():
        h_ref[...] = norm_rows(x_ref[...], g_ref[...])
        meet_partner(partner)
        swap.start()

    t_rows = mm(h_ref[...], w_ref[...]).astype(BF).astype(F32).T

    @pl.when(step < ROPED)
    def _():
        cos, sin = cos_ref[...], sin_ref[...]
        for head in range(FOUR):
            at = HEAD * head
            a, b = t_rows[at:at + HALF], t_rows[at + HALF:at + HEAD]
            out = head_rows(out_ref, head)
            out[:HALF] = (a * cos - b * sin).astype(BF)
            out[HALF:] = (b * cos + a * sin).astype(BF)

    @pl.when(step >= ROPED)
    def _():
        for head in range(FOUR):
            head_rows(out_ref, head)[...] = t_rows[HEAD * head:HEAD * head + HEAD].astype(BF)

    @pl.when(step == PARTS - ONE)
    def _():
        swap.wait()


def qkv_fwd(x, gain, w_qkv, layer, cos_t, sin_t, dest_major, cid):
    oshape = (FOUR, THREE, THREE, HEAD, TOK) if dest_major else (THREE, THREE, FOUR, HEAD, TOK)
    table = spec((HALF, TOK))
    return call(
        qkv_fwd_body, (PARTS,),
        [spec(ALLTOK), spec((ONE, DM)), weight_cols(layer, QT), table, table],
        [spec(ALLTOK), heads_spec(dest_major), ANY],
        [sds(ALLTOK, BF), sds(oshape, BF), sds(ALLTOK, BF)],
        scratch=[DMA, DMA],
        flops=TWO * TOK * DM * THREE * DM, nbytes=8 * MIB, name="qkv_fwd", cid=cid,
    )(x, gain, w_qkv, cos_t, sin_t)


def tile_src(i, *_):
    return i // TWO


def tile_side(i, *_):
    return i % TWO


Q_SPEC = spec((ONE, ONE, THREE, HEAD, QT), tile_src, ZERO, ZERO, ZERO, tile_side)
O_SPEC = spec((ONE, THREE, HEAD, QT), tile_src, ZERO, ZERO, tile_side)
ROW_SPEC = spec((ONE, QT), ZERO, step_of)
STAT_SPEC = spec((8, QT), ZERO, step_of)
GROUP_QKV = (FOUR, THREE, THREE, HEAD, TOK)


def kv_spec(part):
    return spec((FOUR, ONE, THREE, HEAD, TOK), ZERO, part, ZERO, ZERO, ZERO)


def key_tile(kt):
    return kt // TWO, pl.ds(pl.multiple_of((kt % TWO) * QT, QT), QT)


def attn0_fwd_body(lo_s, hi_s, q_ref, k_ref, v_ref, st_ref, en_ref, o_ref, lse_ref, m_s, l_s, acc_s):
    tile = pl.program_id(ZERO)
    m_s[...] = jnp.full(m_s.shape, NEG, F32)
    l_s[...] = jnp.zeros(l_s.shape, F32)
    acc_s[...] = jnp.zeros(acc_s.shape, F32)
    st, en = st_ref[...], en_ref[...]
    io = lax.broadcasted_iota(jnp.int32, (QT, QT), ZERO)
    q_t = [q_ref[ZERO, ZERO, h] * SCALE for h in range(THREE)]

    def body(kt, carry):
        base = kt * QT
        src, cols = key_tile(kt)
        ok = (io >= st - base) & (io < en - base)
        for h in range(THREE):
            row = slice(h, h + ONE)
            k_t = k_ref[src, ZERO, h, :, cols]
            v_t = v_ref[src, ZERO, h, :, cols]
            s = jnp.where(ok, mm_tn(k_t, q_t[h]), NEG)
            m_old = m_s[row]
            m_new = jnp.maximum(m_old, jnp.max(s, axis=ZERO, keepdims=True))
            p = jnp.exp(s - m_new)
            alpha = jnp.exp(m_old - m_new)
            l_s[row] = l_s[row] * alpha + jnp.sum(p, axis=ZERO, keepdims=True)
            acc_s[h] = acc_s[h] * alpha + mm(v_t, p.astype(BF))
            m_s[row] = m_new
        return carry

    lax.fori_loop(lo_s[tile], hi_s[tile], body, ZERO)
    for h in range(THREE):
        row = slice(h, h + ONE)
        o_ref[ZERO, h] = (acc_s[h] / l_s[row]).astype(BF)
        lse_ref[row] = m_s[row] + jnp.log(l_s[row])


def attn0_fwd(lo, hi, qkv, st, en):
    stat = pltpu.VMEM((8, QT), F32)
    return call(
        attn0_fwd_body, (QTILES,),
        [Q_SPEC, kv_spec(ONE), kv_spec(TWO), ROW_SPEC, ROW_SPEC],
        [O_SPEC, STAT_SPEC],
        [sds((FOUR, THREE, HEAD, TOK), BF), sds((8, GRP), F32)],
        scratch=[stat, stat, pltpu.VMEM((THREE, HEAD, QT), F32)],
        prefetch=TWO, flops=TWELVE * GRP * GRP * HEAD, nbytes=6 * MIB, name="attn0_fwd",
    )(lo, hi, qkv, qkv, qkv, st, en)


def attn0_bwd_body(lo_s, hi_s, q_ref, k_ref, v_ref, o_ref, do_ref, lse_ref, st_ref, en_ref, out_ref, dk_s, dv_s, dq_s):
    tile = pl.program_id(ZERO)

    @pl.when(tile == ZERO)
    def _():
        dk_s[...] = jnp.zeros(dk_s.shape, F32)
        dv_s[...] = jnp.zeros(dv_s.shape, F32)

    dq_s[...] = jnp.zeros(dq_s.shape, F32)
    st, en = st_ref[...], en_ref[...]
    io = lax.broadcasted_iota(jnp.int32, (QT, QT), ZERO)
    heads = range(THREE)
    q_t = [q_ref[ZERO, ZERO, h] * SCALE for h in heads]
    do_t = [do_ref[ZERO, h] for h in heads]
    delta = [jnp.sum(do_t[h].astype(F32) * o_ref[ZERO, h].astype(F32), axis=ZERO, keepdims=True) for h in heads]
    lse = [lse_ref[h:h + ONE] for h in heads]

    def body(kt, carry):
        base = kt * QT
        src, cols = key_tile(kt)
        ok = (io >= st - base) & (io < en - base)
        for h in heads:
            k_t = k_ref[src, ZERO, h, :, cols]
            v_t = v_ref[src, ZERO, h, :, cols]
            p = jnp.exp(jnp.where(ok, mm_tn(k_t, q_t[h]) - lse[h], NEG))
            ds = (p * (mm_tn(v_t, do_t[h]) - delta[h])).astype(BF)
            at = (src, h, slice(None), cols)
            dv_s[at] += mm_nt(do_t[h], p.astype(BF))
            dk_s[at] += mm_nt(q_t[h], ds)
            dq_s[h] += mm(k_t, ds)
        return carry

    lax.fori_loop(lo_s[tile], hi_s[tile], body, ZERO)
    src, cols = key_tile(tile)
    for h in heads:
        out_ref[src, ZERO, h, :, cols] = (dq_s[h] * SCALE).astype(BF)

    @pl.when(tile == QTILES - ONE)
    def _():
        for src in range(FOUR):
            for h in heads:
                out_ref[src, ONE, h] = dk_s[src, h].astype(BF)
                out_ref[src, TWO, h] = dv_s[src, h].astype(BF)


def attn0_bwd(lo, hi, qkv, o_t, do_t, lse, st, en):
    acc = pltpu.VMEM((FOUR, THREE, HEAD, TOK), F32)
    return call(
        attn0_bwd_body, (QTILES,),
        [Q_SPEC, kv_spec(ONE), kv_spec(TWO), O_SPEC, O_SPEC, STAT_SPEC, ROW_SPEC, ROW_SPEC],
        spec(GROUP_QKV), sds(GROUP_QKV, BF),
        scratch=[acc, acc, pltpu.VMEM((THREE, HEAD, QT), F32)],
        prefetch=TWO, flops=30 * GRP * GRP * HEAD, nbytes=TWELVE * MIB, name="attn0_bwd",
    )(lo, hi, qkv, qkv, qkv, o_t, do_t, lse, st, en)


NBLK = TOK // LANE
EXT = TOK + TWO * LANE


def own_head(part):
    return spec((ONE, HEAD, TOK), lambda n: NHEAD * part + n, ZERO, ZERO)


def halo_head(part):
    return spec((ONE, HEAD, LANE), lambda n: NHEAD * part + n, ZERO, ZERO)


def joined(left, mid, right):
    return jnp.concatenate([left[ZERO], mid[ZERO], right[ZERO]], axis=ONE)


def blocks(first, last):
    return slice(LANE * first, LANE * last)


def in_bounds(lo_ref, hi_ref, blk, first, last):
    io = lax.broadcasted_iota(jnp.int32, (LANE * (last - first), LANE), ZERO) + LANE * first
    cols = blocks(blk, blk + ONE)
    return (io >= lo_ref[:, cols]) & (io < hi_ref[:, cols])


def attn1_fwd_body(q_ref, k_ref, v_ref, kl_ref, vl_ref, kr_ref, vr_ref, lo_ref, hi_ref, o_ref, lse_ref):
    q_t = q_ref[ZERO] * SCALE
    k_t = joined(kl_ref, k_ref, kr_ref)
    v_t = joined(vl_ref, v_ref, vr_ref)
    for i in range(NBLK):
        cols, wide = blocks(i, i + ONE), blocks(i, i + THREE)
        s = jnp.where(in_bounds(lo_ref, hi_ref, i + ONE, i, i + THREE), mm_tn(k_t[:, wide], q_t[:, cols]), NEG)
        m = jnp.max(s, axis=ZERO, keepdims=True)
        e = jnp.exp(s - m)
        l = jnp.sum(e, axis=ZERO, keepdims=True)
        o_ref[ZERO, :, cols] = mm(v_t[:, wide], (e / l).astype(BF)).astype(BF)
        lse_ref[ZERO, :, cols] = m + jnp.log(l)


def attn1_fwd(qkv, left, right, lo, hi):
    bound = spec((ONE, EXT))
    return call(
        attn1_fwd_body, (NHEAD,),
        [own_head(ZERO), own_head(ONE), own_head(TWO), halo_head(ZERO), halo_head(ONE), halo_head(ZERO), halo_head(ONE),
         bound, bound],
        [own_head(ZERO), spec((ONE, ONE, TOK), step_of, ZERO, ZERO)],
        [sds((NHEAD, HEAD, TOK), BF), sds((NHEAD, ONE, TOK), F32)],
        flops=NHEAD * FOUR * TOK * EXT * HALF, nbytes=FOUR * MIB, name="attn1_fwd",
    )(qkv, qkv, qkv, left, left, right, right, lo, hi)


def attn1_bwd_body(q_ref, k_ref, v_ref, do_ref, kl_ref, vl_ref, kr_ref, vr_ref, ql_ref, dl_ref, qr_ref, dr_ref,
                   lse_ref, del_ref, lo_ref, hi_ref, out_ref):
    q_t = joined(ql_ref, q_ref, qr_ref) * SCALE
    do_t = joined(dl_ref, do_ref, dr_ref)
    k_t = joined(kl_ref, k_ref, kr_ref)
    v_t = joined(vl_ref, v_ref, vr_ref)
    last_own = NBLK + ONE
    dk = [jnp.zeros((HEAD, LANE), F32) for _ in range(last_own)]
    dv = [jnp.zeros((HEAD, LANE), F32) for _ in range(last_own)]
    for e in range(NBLK + TWO):
        mine = ONE <= e <= NBLK
        first = e - ONE if mine else max(e - ONE, ONE)
        last = e + TWO if mine else min(e + TWO, last_own)
        cols, wide = blocks(e, e + ONE), blocks(first, last)
        ok = in_bounds(lo_ref, hi_ref, e, first, last)
        p = jnp.exp(jnp.where(ok, mm_tn(k_t[:, wide], q_t[:, cols]) - lse_ref[ZERO, :, cols], NEG))
        ds = jnp.where(ok, p * (mm_tn(v_t[:, wide], do_t[:, cols]) - del_ref[ZERO, :, cols]), F32(ZERO)).astype(BF)
        p_bf = p.astype(BF)
        if mine:
            out_ref[ZERO, ZERO, :, blocks(e - ONE, e)] = (mm(k_t[:, wide], ds) * SCALE).astype(BF)
        for kb in range(max(first, ONE), min(last, last_own)):
            rows = blocks(kb - first, kb - first + ONE)
            dv[kb] += mm_nt(do_t[:, cols], p_bf[rows])
            dk[kb] += mm_nt(q_t[:, cols], ds[rows])
    for kb in range(ONE, last_own):
        out_ref[ONE, ZERO, :, blocks(kb - ONE, kb)] = dk[kb].astype(BF)
        out_ref[TWO, ZERO, :, blocks(kb - ONE, kb)] = dv[kb].astype(BF)


def attn1_bwd(qkv, do_t, left, right, dleft, dright, lse_x, del_x, lo, hi):
    stat = spec((ONE, ONE, EXT), step_of, ZERO, ZERO)
    bound = spec((ONE, EXT))
    pair = [halo_head(ZERO), halo_head(ONE)]
    return call(
        attn1_bwd_body, (NHEAD,),
        [own_head(ZERO), own_head(ONE), own_head(TWO), own_head(ZERO)] + pair * FOUR + [stat, stat, bound, bound],
        spec((THREE, ONE, HEAD, TOK), ZERO, step_of, ZERO, ZERO),
        sds((THREE, NHEAD, HEAD, TOK), BF),
        flops=NHEAD * 10 * TOK * EXT * HALF, nbytes=8 * MIB, name="attn1_bwd",
    )(qkv, qkv, qkv, do_t, left, left, right, right, dleft, dleft, dright, dright, lse_x, del_x, lo, hi)


RB = 256
ROWBLK = [slice(r, r + RB) for r in range(ZERO, TOK, RB)]
HALFT = NFT // TWO
SQRT_HALF = math.sqrt(SCALE * FOUR)
PDF_SCALE = SQRT_HALF / math.sqrt(math.pi)
UBLK = (TWO, TOK, FT)
U_SPEC = spec(UBLK, ZERO, ZERO, step_of)


def normal_cdf(a):
    return SQRT_HALF * SQRT_HALF * (ONE + lax.erf(a * SQRT_HALF))


def att_block(ref, n):
    return ref.at[n % FOUR, n // FOUR] if ref.shape[ZERO] == FOUR else ref.at[n]


def half_rows(ref, which):
    n = ref.shape[ZERO] // TWO
    return ref.at[pl.ds(pl.multiple_of(which * n, n), n)]


def mlp_fwd_body(x_ref, o_ref, wp_ref, g_ref, wa_ref, wb_ref, wo_ref, x1_ref, h_ref, u_ref, m_ref, y_ref, of_ref,
                 mr_ref, hr_ref, or_ref, acc, m_s, ssem, rsem):
    step = pl.program_id(ZERO)
    core, partner = core_and_partner()
    other = ONE - core

    def send(n, src, dst):
        return to_partner(partner, src, dst, ssem.at[n], rsem.at[n])

    small = [send(HALFT, h_ref, hr_ref), send(HALFT + ONE, half_rows(of_ref, other), or_ref)]

    @pl.when(step == ZERO)
    def _():
        for n in range(NHEAD):
            of_ref[HEAD * n:HEAD * n + HEAD, :] = att_block(o_ref, n)[...]
        x1 = (x_ref[...].astype(F32) + mm_tn(of_ref[...], wp_ref[...])).astype(BF)
        x1_ref[...] = x1
        h_ref[...] = norm_rows(x1, g_ref[...])
        acc[...] = x1.astype(F32)
        meet_partner(partner)
        for cp in small:
            cp.start()

    slot = lax.rem(step, HALFT)
    for rows in ROWBLK:
        ua = mm(h_ref[rows], wa_ref[...]).astype(BF)
        ub = mm(h_ref[rows], wb_ref[...]).astype(BF)
        u_ref[ZERO, rows] = ua
        u_ref[ONE, rows] = ub
        a = ua.astype(F32)
        m = ((a * normal_cdf(a)) * ub.astype(F32)).astype(BF)
        m_ref[rows] = m
        acc[rows] += mm(m, wo_ref[...])

    @pl.when(step // HALFT == other)
    def _():
        m_s[slot] = m_ref[...]
        send(slot, m_s.at[slot], mr_ref.at[slot]).start()

    @pl.when(step == NFT - ONE)
    def _():
        y_ref[...] = acc[...].astype(BF)
        for n in range(HALFT):
            send(n, m_s.at[n], mr_ref.at[n]).wait()
        for cp in small:
            cp.wait()


def proj_spec(layer):
    return spec((None, DM, DM), layer, ZERO, ZERO)


def out_weight(layer):
    return spec((None, FT, DM), layer, step_of, ZERO)


def mlp_fwd(x, o_t, w_proj, gain, w_in, w_out, layer, cid):
    half_m = (HALFT, TOK, FT)
    toks = sds(ALLTOK, BF)
    return call(
        mlp_fwd_body, (NFT,),
        [spec(ALLTOK), spec(o_t.shape), proj_spec(layer), spec((ONE, DM)),
         weight_cols(layer, FT), weight_cols(layer, FT, NFT), out_weight(layer)],
        [spec(ALLTOK), spec(ALLTOK), U_SPEC, spec((TOK, FT), ZERO, step_of), spec(ALLTOK), spec((DM, TOK)), ANY, ANY, ANY],
        [toks, toks, sds((TWO, TOK, FF), BF), sds((TOK, FF), BF), toks, sds((DM, TOK), BF),
         sds(half_m, BF), toks, sds((DM // TWO, TOK), BF)],
        scratch=[pltpu.VMEM(ALLTOK, F32), pltpu.VMEM(half_m, BF), DMA((HALFT + TWO,)), DMA((HALFT + TWO,))],
        flops=TWO * TOK * DM * (DM + THREE * FF), nbytes=26 * MIB, name="mlp_fwd", cid=cid,
    )(x, o_t, w_proj, gain, w_in, w_in, w_out)


STATS = 16


def mlp_bwd_body(dy_ref, x1_ref, g_ref, wa_ref, wb_ref, wo_ref, u_ref, wp_ref, of_ref,
                 du_ref, dmid_ref, gg_ref, dot_ref, del_ref, dur_ref, dyr_ref, dmr_ref, acc, du_s, ssem, rsem):
    step = pl.program_id(ZERO)
    core, partner = core_and_partner()

    def send(n, src, dst):
        return to_partner(partner, src, dst, ssem.at[n], rsem.at[n])

    def send_du(n):
        return send(n, du_s.at[n], dur_ref.at[:, pl.ds(pl.multiple_of(n * FT, FT), FT)])

    send_dy = send(NFT, dy_ref, dyr_ref)
    send_dmid = send(NFT + ONE, dmid_ref, dmr_ref)

    @pl.when(step == ZERO)
    def _():
        acc[...] = jnp.zeros(acc.shape, F32)
        meet_partner(partner)
        send_dy.start()

    for rows in ROWBLK:
        dm = mm_nt(dy_ref[rows], wo_ref[...]).astype(BF).astype(F32)
        a = u_ref[ZERO, rows].astype(F32)
        b = u_ref[ONE, rows].astype(F32)
        cdf = normal_cdf(a)
        pdf = jnp.exp(a * a * (SCALE * FOUR - ONE)) * PDF_SCALE
        db = (dm * (a * cdf)).astype(BF)
        da = (dm * b * (cdf + a * pdf)).astype(BF)
        du_ref[ZERO, rows] = da
        du_ref[ONE, rows] = db
        acc[rows] += mm_nt(da, wa_ref[...]) + mm_nt(db, wb_ref[...])

    du_s[step] = du_ref[ONE - core]
    send_du(step).start()

    @pl.when(step == NFT - ONE)
    def _():
        d_ln, gg = norm_rows_grad(x1_ref[...], g_ref[...], acc[...].astype(BF))
        gg_ref[...] = gg
        d_mid = add_bf(dy_ref[...], d_ln)
        dmid_ref[...] = d_mid
        send_dmid.start()
        d_att = mm_nt(wp_ref[...], d_mid).astype(BF)
        for n in range(NHEAD):
            rows = slice(HEAD * n, HEAD * n + HEAD)
            blk = d_att[rows]
            att_block(dot_ref, n)[...] = blk
            del_ref[n:n + ONE, :] = jnp.sum(blk.astype(F32) * of_ref[rows].astype(F32), axis=ZERO, keepdims=True)
        del_ref[NHEAD:, :] = jnp.zeros((STATS - NHEAD, TOK), F32)
        for n in range(NFT):
            send_du(n).wait()
        send_dy.wait()
        send_dmid.wait()


def mlp_bwd(dy, x1, gain, w_in, w_out, u, w_proj, o_flat, layer, oshape, cid):
    du_half = (NFT, TOK, FT)
    toks = sds(ALLTOK, BF)
    return call(
        mlp_bwd_body, (NFT,),
        [spec(ALLTOK), spec(ALLTOK), spec((ONE, DM)), weight_cols(layer, FT), weight_cols(layer, FT, NFT),
         out_weight(layer), U_SPEC, proj_spec(layer), spec((DM, TOK))],
        [U_SPEC, spec(ALLTOK), spec((ONE, DM)), spec(oshape), spec((STATS, TOK)), ANY, ANY, ANY],
        [sds((TWO, TOK, FF), BF), toks, sds((ONE, DM), F32), sds(oshape, BF), sds((STATS, TOK), F32),
         sds((TOK, FF), BF), toks, toks],
        scratch=[pltpu.VMEM(ALLTOK, F32), pltpu.VMEM(du_half, BF), DMA((NFT + TWO,)), DMA((NFT + TWO,))],
        flops=TWO * TOK * DM * (DM + THREE * FF), nbytes=30 * MIB, name="mlp_bwd", cid=cid,
    )(dy, x1, gain, w_in, w_in, w_out, u, w_proj, o_flat)


def qkv_bwd_body(d_ref, cos_ref, sin_ref, w_ref, x_ref, g_ref, dmid_ref, dt_ref, dx_ref, gg_ref, dtr_ref,
                 acc, dt_s, ssem, rsem):
    step = pl.program_id(ZERO)
    core, partner = core_and_partner()

    def send(n):
        return to_partner(partner, dt_s.at[n, ONE - core], dtr_ref.at[pl.ds(pl.multiple_of(n * LANE, LANE), LANE)],
                          ssem.at[n], rsem.at[n])

    @pl.when(step == ZERO)
    def _():
        acc[...] = jnp.zeros(acc.shape, F32)
        meet_partner(partner)

    def put(head, row, val):
        at = row + HEAD * (head % TWO)
        dt_s[step, head // TWO, at:at + val.shape[ZERO]] = val

    @pl.when(step < ROPED)
    def _():
        cos, sin = cos_ref[...], sin_ref[...]
        for head in range(FOUR):
            d_head = head_rows(d_ref, head)[...].astype(F32)
            da, db = d_head[:HALF], d_head[HALF:]
            put(head, ZERO, (da * cos + db * sin).astype(BF))
            put(head, HALF, (db * cos - da * sin).astype(BF))

    @pl.when(step >= ROPED)
    def _():
        for head in range(FOUR):
            put(head, ZERO, head_rows(d_ref, head)[...])

    send(step).start()
    dt = dt_s[step]
    dt_ref[...] = dt
    acc[...] += mm(w_ref[...], dt.reshape(QT, TOK))

    @pl.when(step == PARTS - ONE)
    def _():
        d_ln, gg = norm_rows_grad(x_ref[...], g_ref[...], acc[...].T.astype(BF))
        gg_ref[...] = gg
        dx_ref[...] = add_bf(dmid_ref[...], d_ln)
        for n in range(PARTS):
            send(n).wait()


def qkv_bwd(d_qkv, cos_t, sin_t, w_qkv, x, gain, d_mid, layer, dest_major, cid):
    table = spec((HALF, TOK))
    feats = PARTS * LANE
    return call(
        qkv_bwd_body, (PARTS,),
        [heads_spec(dest_major), table, table, weight_cols(layer, QT), spec(ALLTOK), spec((ONE, DM)), spec(ALLTOK)],
        [spec((TWO, LANE, TOK), ZERO, step_of, ZERO), spec(ALLTOK), spec((ONE, DM)), ANY],
        [sds((TWO, feats, TOK), BF), sds(ALLTOK, BF), sds((ONE, DM), F32), sds((feats, TOK), BF)],
        scratch=[pltpu.VMEM((DM, TOK), F32), pltpu.VMEM((PARTS, TWO, LANE, TOK), BF), DMA((PARTS,)), DMA((PARTS,))],
        flops=TWO * TOK * DM * THREE * DM, nbytes=10 * MIB, name="qkv_bwd", cid=cid,
    )(d_qkv, cos_t, sin_t, w_qkv, x, gain, d_mid)


DOWN = FF // TWO
UP = FF
PROJ = DM // TWO
QKV = PARTS * LANE
LAYER_ROWS = DOWN + UP + PROJ + QKV
ALLROWS = TWO * LAYER_ROWS
NDOWN = DOWN // RB
NK = DM // RB


def up_step(s):
    return jnp.maximum(s - NDOWN, ZERO)


def down_step(s):
    return jnp.minimum(s, NDOWN - ONE)


def grad_mlp_body(core_s, g_ref, ma, mb, dya, dyb, ha, hb, dua, dub, out_ref):
    step = pl.program_id(ZERO)

    @pl.when(step < NDOWN)
    def _():
        out_ref[...] = mm_tn(ma[...], dya[...]) + mm_tn(mb[...], dyb[...])

    @pl.when(step >= NDOWN)
    def _():
        out_ref[...] = mm_tn(ha[...], dua[...]) + mm_tn(hb[...], dub[...])


def grad_call(body, core, grads, steps, in_specs, args, rows, first):
    shared = [] if grads is None else [grads]
    return call(
        body, (steps,), [ANY] * len(shared) + in_specs,
        spec((rows, DM), lambda s, c: first + s, ZERO), sds((ALLROWS, DM), F32),
        prefetch=ONE, flops=FOUR * steps * rows * TOK * DM, nbytes=20 * MIB, name=body.__name__,
        alias={ONE: ZERO} if shared else None,
    )(core, *shared, *args)


def grad_mlp_body(core_s, *refs):
    ma, mb, dya, dyb, ha, hb, dua, dub, out_ref = refs[-PARTS:]
    step = pl.program_id(ZERO)

    @pl.when(step < NDOWN)
    def _():
        out_ref[...] = mm_tn(ma[...], dya[...]) + mm_tn(mb[...], dyb[...])

    @pl.when(step >= NDOWN)
    def _():
        out_ref[...] = mm_tn(ha[...], dua[...]) + mm_tn(hb[...], dub[...])


def grad_mlp(core, grads, m, m_r, dy, dy_r, h, h_r, du, du_r, first_row):
    per_ft = FT // RB
    toks = spec(ALLTOK)
    hcol = spec((TOK, RB), ZERO, lambda s, c: up_step(s) % NK)
    col = lambda s, *_: up_step(s) // NK
    return grad_call(
        grad_mlp_body, core, grads, NDOWN + UP // RB,
        [spec((TOK, RB), ZERO, lambda s, c: NDOWN * c[ZERO] + down_step(s)),
         spec((None, TOK, RB), lambda s, c: down_step(s) // per_ft, ZERO, lambda s, c: down_step(s) % per_ft),
         toks, toks, hcol, hcol,
         spec((None, TOK, DM), lambda s, c: c[ZERO], ZERO, col), spec(ALLTOK, ZERO, col)],
        (m, m_r, dy, dy_r, h, h_r, du, du_r), RB, first_row // RB)


def grad_att_body(core_s, *refs):
    oa, ob, dma, dmb, ta, tb, ha, hb, out_ref = refs[-PARTS:]
    step = pl.program_id(ZERO)

    @pl.when(step == ZERO)
    def _():
        out_ref[...] = mm(oa[...], dma[...]) + mm(ob[...], dmb[...])

    @pl.when(step > ZERO)
    def _():
        out_ref[...] = mm(ta[...], ha[...]) + mm(tb[...], hb[...])


def grad_att(core, grads, of, of_r, dmid, dmid_r, dt, dt_r, h, h_r, first_row):
    toks = spec(ALLTOK)
    blk = (PROJ, TOK)
    qkv_step = lambda s, *_: jnp.maximum(s - ONE, ZERO)
    return grad_call(
        grad_att_body, core, grads, ONE + QKV // PROJ,
        [spec(blk, lambda s, c: c[ZERO], ZERO), spec(blk), toks, toks,
         spec((None,) + blk, lambda s, c: c[ZERO], qkv_step, ZERO), spec(blk, qkv_step, ZERO), toks, toks],
        (of, of_r, dmid, dmid_r, dt, dt_r, h, h_r), PROJ, (first_row + DOWN + UP) // PROJ)


NB, NS, CH, SB, LF = 4, 6, 128, 32, 8
RS = PARTS
LAST = RS + RS


def ring_body(g_ref, ln_ref, f_ref, lnout_ref, bufa, bufb, bufc, gath, stage, lnbuf,
              ssem, rsem, psem, qsem, csem, stsem, lns, lnr):
    core, partner = core_and_partner()
    dp = lax.axis_index('dp')
    pos = (lax.axis_index('sp'), lax.rem(dp // TWO, FOUR), dp // 8)
    streams = [(c, sg) for c in range(THREE) for sg in (ONE, -ONE)]
    bufs, sizes = (bufa, bufb, bufc), (CH, SB, LF)
    peers = range(ONE, FOUR)

    def mod4(v):
        return lax.rem(v + 8, FOUR)

    def at(axis, val):
        if axis == ZERO:
            return {'sp': val}
        yz = (val, pos[TWO]) if axis == ONE else (pos[ONE], val)
        return {'dp': yz[ONE] * 8 + yz[ZERO] * TWO + core}

    def shifted(axis, d):
        return at(axis, mod4(pos[axis] + d))

    def axis_of(s, ph):
        return (streams[s][ZERO] + ph) % THREE

    def idx(s, ph, t):
        return mod4(pos[axis_of(s, ph)] - streams[s][ONE] * t)

    def own(s, ph):
        return idx(s, ph, -ONE)

    def base(b, s):
        return (b * NS + s) * (FOUR * CH)

    bar = pltpu.get_barrier_semaphore()
    for ax in range(THREE):
        for d in peers:
            pl.semaphore_signal(bar, inc=ONE, device_id=shifted(ax, d), device_id_type=MESH)
    pl.semaphore_signal(bar, inc=ONE, device_id=partner, device_id_type=MESH)
    pl.semaphore_wait(bar, 10)

    def rows(ref, start, n):
        return ref.at[pl.ds(pl.multiple_of(start, LF), n)]

    def frows(start, n):
        return f_ref.at[core, pl.ds(pl.multiple_of(start, LF), n)]

    def same_bytes(b, k):
        if k < RS:
            return bufs[k // THREE].at[b, k % THREE]
        n = sizes[TWO - (k - RS) // THREE]
        return gath.at[b] if n == CH else gath.at[b, :, pl.ds(ZERO, n)]

    def wait_for(ref, sem):
        pltpu.make_async_copy(ref, ref, sem).wait()

    def send(b, s, k):
        ph = k // THREE if k < RS else TWO - (k - RS) // THREE
        t = k % THREE
        n = sizes[ph]
        if k < RS:
            dst = bufs[ph].at[b, t, s]
            if t:
                src = bufs[ph].at[b, t - ONE, s]
            elif ph:
                src = rows(bufs[ph - ONE].at[b, TWO, s], idx(s, ph, ZERO) * n, n)
            else:
                src = rows(g_ref, base(b, s) + idx(s, ZERO, ZERO) * n, n)
        elif ph:
            off = own(s, ONE) * SB if ph == TWO else ZERO
            src = dst = rows(gath.at[b, s], off + idx(s, ph, t - ONE) * n, n)
        else:
            dst = frows(base(b, s) + idx(s, ZERO, t - ONE) * n, n)
            src = dst if t else gath.at[b, s]
        pltpu.make_async_remote_copy(src_ref=src, dst_ref=dst, send_sem=ssem.at[b, k], recv_sem=rsem.at[b, k],
                                     device_id=shifted(axis_of(s, ph), streams[s][ONE]), device_id_type=MESH).start()

    def stage_load(n):
        t, b, slot = n // NB, lax.rem(n, NB), lax.rem(n, TWO)
        for s in range(NS):
            pltpu.make_async_copy(rows(g_ref, base(b, s) + idx(s, ZERO, t + ONE) * CH, CH), stage.at[slot, s],
                                  stsem.at[slot]).start()

    def ln_copy(ph, d):
        return pltpu.make_async_remote_copy(
            src_ref=lnbuf.at[ph, THREE] if ph else ln_ref, dst_ref=lnbuf.at[ph, d - ONE], send_sem=lns.at[ph, d - ONE],
            recv_sem=lnr.at[ph, d - ONE], device_id=shifted(ph, d) if ph < THREE else partner, device_id_type=MESH)

    def ln_sum(ph):
        vals = [lnbuf[ph, THREE] if ph else ln_ref[...]] + [lnbuf[ph, d - ONE] for d in peers]
        total = jnp.zeros_like(vals[ZERO])
        for p in range(FOUR):
            term = vals[ZERO]
            for d in peers:
                term = jnp.where(mod4(pos[ph] - d) == p, vals[d], term)
            total = total + term
        return total

    def batches(fn, start=ZERO):
        def body(b, c):
            fn(b)
            return c
        lax.fori_loop(start, NB, body, ZERO)

    def first(b):
        for s in range(NS):
            send(b, s, ZERO)

    first(ZERO)
    stage_load(jnp.int32(ZERO))
    for d in peers:
        ln_copy(ZERO, d).start()
    batches(first, ONE)

    for k in range(RS):
        ph, t = k // THREE, k % THREE
        buf, size = bufs[ph], sizes[ph]

        def step(b, k=k, ph=ph, t=t, buf=buf, size=size):
            n = k * NB + b
            slot = lax.rem(n, TWO)
            if not ph:
                @pl.when(n < THREE * NB - ONE)
                def _():
                    stage_load(n + ONE)
                wait_for(stage.at[slot], stsem.at[slot])
            wait_for(same_bytes(b, k), rsem.at[b, k])
            for s in range(NS):
                if ph:
                    off = pl.multiple_of(idx(s, ph, t + ONE) * size, LF)
                    buf[b, t, s] += bufs[ph - ONE][b, TWO, s, pl.ds(off, size)]
                else:
                    @pl.loop(ZERO, CH, step=SB)
                    def _(r):
                        at_r = pl.ds(pl.multiple_of(r, SB), SB)
                        buf[b, t, s, at_r] += stage[slot, s, at_r]
                if k == RS - ONE:
                    off = pl.multiple_of(own(s, ONE) * SB + own(s, TWO) * LF, LF)
                    gath[b, s, pl.ds(off, LF)] = bufc[b, TWO, s]
                send(b, s, k + ONE)

        batches(step)
        if k < SIX and k % TWO == ZERO:
            lp = k // TWO
            for d in peers:
                ln_copy(lp, d).wait()
            lnbuf[lp + ONE, THREE] = ln_sum(lp)
            for d in peers if lp < TWO else (ONE,):
                ln_copy(lp + ONE, d).start()

    def hand_over(b, s, j, src, start):
        pltpu.make_async_remote_copy(src_ref=src, dst_ref=frows(start, CH), send_sem=psem.at[b, j], recv_sem=qsem.at[b, j],
                                     device_id=partner, device_id_type=MESH).start()

    for k in range(RS, LAST):
        def step(b, k=k):
            wait_for(same_bytes(b, k), rsem.at[b, k])
            piece = k - (LAST - FOUR)
            for s in range(NS):
                if k < LAST - ONE:
                    send(b, s, k + ONE)
                if piece >= ZERO:
                    start = base(b, s) + idx(s, ZERO, piece - ONE) * CH
                    if piece:
                        hand_over(b, s, piece, frows(start, CH), start)
                    else:
                        pltpu.make_async_copy(gath.at[b, s], frows(start, CH), csem.at[b]).start()
                        hand_over(b, s, piece, gath.at[b, s], start)
        batches(step)

    ln_copy(THREE, ONE).wait()
    lnout_ref[...] = lnbuf[THREE, THREE] + lnbuf[THREE, ZERO]

    def finish(b):
        for k in range(LAST):
            wait_for(same_bytes(b, k), ssem.at[b, k])
        for j in range(FOUR):
            wait_for(gath.at[b], psem.at[b, j])
            wait_for(gath.at[b], qsem.at[b, j])
        wait_for(gath.at[b], csem.at[b])
    batches(finish)


def ring_all_reduce(g, ln, cid):
    vmem = pl.BlockSpec(memory_space=pltpu.VMEM)
    return pl.pallas_call(
        ring_body,
        in_specs=[ANY, vmem],
        out_specs=[ANY, vmem],
        out_shape=[sds((TWO, ALLROWS, DM), F32), sds(ln.shape, F32)],
        scratch_shapes=[
            pltpu.VMEM((NB, THREE, NS, CH, DM), F32), pltpu.VMEM((NB, THREE, NS, SB, DM), F32),
            pltpu.VMEM((NB, THREE, NS, LF, DM), F32), pltpu.VMEM((NB, NS, CH, DM), F32), pltpu.VMEM((TWO, NS, CH, DM), F32),
            pltpu.VMEM((FOUR, FOUR) + ln.shape, F32),
            DMA((NB, LAST)), DMA((NB, LAST)), DMA((NB, FOUR)), DMA((NB, FOUR)), DMA((NB,)), DMA((TWO,)),
            DMA((FOUR, THREE)), DMA((FOUR, THREE)),
        ],
        compiler_params=pltpu.CompilerParams(collective_id=cid, has_side_effects=True, vmem_limit_bytes=63 * MIB),
        name="ring_all_reduce",
    )(g, ln)


def copy_body(in_ref, out_ref):
    out_ref[...] = in_ref[...]


def turn_body(a_ref, b_ref, out_ref):
    out_ref[ZERO, :, :LANE] = a_ref[ZERO].T
    out_ref[ZERO, :, LANE:] = b_ref[ZERO].T


def unpack(f):
    def blk(rows, row0):
        return (ONE, rows, DM), (lambda l, *_: (ONE - l) * (LAYER_ROWS // rows) + row0 // rows)

    whole, at_layer = blk(DM, ZERO)
    core_of = lambda l, c, *_: c
    layer_of = lambda l, *_: l
    nbytes = 100 * MIB
    g_out = call(copy_body, (TWO, TWO, TWO),
                 [spec(whole, core_of, lambda l, c, i: at_layer(l) + i, ZERO)],
                 spec(whole, layer_of, lambda l, c, i: TWO * c + i, ZERO), sds((TWO, FF, DM), F32), nbytes=nbytes)(f)
    g_in = call(copy_body, (TWO, TWO, FOUR),
                [spec(whole, core_of, lambda l, c, j: at_layer(l) + TWO + j, ZERO)],
                spec(whole, layer_of, ZERO, lambda l, c, j: FOUR * c + j), sds((TWO, DM, TWO * FF), F32), nbytes=nbytes)(f)
    half, at_proj = blk(PROJ, DOWN + UP)
    g_proj = call(copy_body, (TWO, TWO), [spec(half, core_of, at_proj, ZERO)], spec(half, layer_of, core_of, ZERO),
                  sds((TWO, DM, DM), F32), nbytes=nbytes)(f)
    lane, at_qkv = blk(LANE, DOWN + UP + PROJ)
    row = lambda l, s: at_qkv(l) + s
    g_qkv = call(turn_body, (TWO, PARTS), [spec(lane, ZERO, row, ZERO), spec(lane, ONE, row, ZERO)],
                 spec((ONE, DM, QT), layer_of, ZERO, lambda l, s: s), sds((TWO, DM, THREE * DM), F32), nbytes=nbytes)(f, f)
    return g_qkv, g_proj, g_in, g_out


def rope_tables(pos, base):
    inv_freq = base ** (jnp.arange(HALF).astype(F32) * (-TWO / HEAD))
    angles = inv_freq[:, None] * pos.astype(F32)[None, :]
    return jnp.cos(angles), jnp.sin(angles)


def solution(mesh):
    token_spec = P(('dp', 'sp'), None)
    n_sp = mesh.shape['sp']
    to_right = [(i, i + ONE) for i in range(n_sp - ONE)]
    to_left = [(i + ONE, i) for i in range(n_sp - ONE)]
    cids = list(range(PARTS))

    def halo_swap(arr):
        from_left = lax.ppermute(arr[..., TOK - LANE:], 'sp', to_right)
        from_right = lax.ppermute(arr[..., :LANE], 'sp', to_left)
        return from_left, from_right

    def exchange(arr):
        return lax.all_to_all(arr, 'sp', ZERO, ZERO, tiled=True)

    def device_step(x_loc, cu_loc, pos_loc, w_qkv, w_proj, w_in, w_out, ln_attn, ln_mlp, d_out):
        sp = lax.axis_index('sp')
        core = (lax.axis_index('dp') % TWO).reshape(ONE)
        cu = cu_loc[ZERO][:, None]

        def bounds_of(tok):
            start = jnp.max(jnp.where(cu <= tok, cu, ZERO), axis=ZERO)
            return start, jnp.min(jnp.where(cu > tok, cu, GRP), axis=ZERO)

        start, stop = bounds_of(jnp.arange(GRP)[None, :])
        tiles = start[::QT] // QT, (stop[QT - ONE::QT] + QT - ONE) // QT
        rows = start[None, :], stop[None, :]
        shift = sp * TOK - LANE
        tok_x = jnp.arange(EXT) + shift
        start_x, stop_x = bounds_of(tok_x[None, :])
        inside = (tok_x >= ZERO) & (tok_x < GRP)
        near = (jnp.where(inside, jnp.maximum(start_x, tok_x - WIN) - shift, ZERO)[None, :],
                jnp.where(inside, jnp.minimum(stop_x, tok_x + WIN + ONE) - shift, ZERO)[None, :])
        tab0, tab1 = [rope_tables(pos_loc, base) for base in BASES]
        la0, la1, lm0, lm1 = ln_attn[:ONE], ln_attn[ONE:], ln_mlp[:ONE], ln_mlp[ONE:]
        per_head = (NHEAD, HEAD, TOK)

        h0, qkv0, h0r = qkv_fwd(x_loc, la0, w_qkv, ZERO, *tab0, True, cids[ONE])
        qkv0 = exchange(qkv0)
        oh0, lse0 = attn0_fwd(*tiles, qkv0, *rows)
        x01, h02, u0, m0, x1, of0, m0r, h02r, of0r = mlp_fwd(x_loc, exchange(oh0), w_proj, lm0, w_in, w_out, ZERO, cids[TWO])
        h1, qkv1, h1r = qkv_fwd(x1, la1, w_qkv, ONE, *tab1, False, cids[THREE])
        qkv1 = qkv1.reshape((THREE * NHEAD, HEAD, TOK))
        kv_halo = halo_swap(qkv1[NHEAD:])
        o1, lse1 = attn1_fwd(qkv1, *kv_halo, *near)
        x11, h12, u1, m1, y, of1, m1r, h12r, of1r = mlp_fwd(x1, o1, w_proj, lm1, w_in, w_out, ONE, cids[FOUR])
        du1, dmid1, ggm1, do1, del1, du1r, dy1r, dmid1r = mlp_bwd(
            d_out, x11, lm1, w_in, w_out, u1, w_proj, of1, ONE, per_head, cids[5])
        d_halo = halo_swap(jnp.concatenate([qkv1[:NHEAD], do1], axis=ZERO))
        stats = jnp.concatenate([lse1.reshape(NHEAD, TOK), del1[:NHEAD]], axis=ZERO)
        from_left, from_right = halo_swap(stats)
        lse_x, del_x = jnp.concatenate([from_left, stats, from_right], axis=ONE).reshape(TWO, NHEAD, ONE, EXT)
        dqkv1 = attn1_bwd(qkv1, do1, *kv_halo, *d_halo, lse_x, del_x, *near)
        dt1, dx1, gga1, dt1r = qkv_bwd(dqkv1.reshape(THREE, THREE, FOUR, HEAD, TOK), *tab1, w_qkv, x1, la1, dmid1,
                                       ONE, False, cids[SIX])
        grads = grad_mlp(core, None, m1, m1r, d_out, dy1r, h12, h12r, du1, du1r, ZERO)
        grads = grad_att(core, grads, of1, of1r, dmid1, dmid1r, dt1, dt1r, h1, h1r, ZERO)
        du0, dmid0, ggm0, do0, _, du0r, dy0r, dmid0r = mlp_bwd(
            dx1, x01, lm0, w_in, w_out, u0, w_proj, of0, ZERO, oh0.shape, cids[7])
        grads = grad_mlp(core, grads, m0, m0r, dx1, dy0r, h02, h02r, du0, du0r, LAYER_ROWS)
        dqkv0 = exchange(attn0_bwd(*tiles, qkv0, oh0, exchange(do0), lse0, *rows))
        dt0, dx0, gga0, dt0r = qkv_bwd(dqkv0, *tab0, w_qkv, x_loc, la0, dmid0, ZERO, True, cids[8])
        grads = grad_att(core, grads, of0, of0r, dmid0, dmid0r, dt0, dt0r, h0, h0r, LAYER_ROWS)

        gains = jnp.concatenate([gga0, gga1, ggm0, ggm1, jnp.zeros((FOUR, DM), F32)], axis=ZERO)
        summed, gains = ring_all_reduce(grads, gains, cids[ZERO])
        return (y, dx0) + unpack(summed) + (gains[:TWO], gains[TWO:FOUR])

    in_specs = (token_spec, P('dp', None), P(('dp', 'sp'))) + (P(),) * SIX + (token_spec,)
    out_specs = (token_spec, token_spec) + (P(),) * SIX
    return jax.shard_map(device_step, mesh=mesh, in_specs=in_specs, out_specs=out_specs, check_vma=False)
```

time: 1490 us -> 789 us (0.53)
  Pallas kernels: 0 us -> 676 us
  matrix products: 437 us -> 0 us
  waiting for transfers between devices: 441 us -> 43.9 us
  local copies, waits for them, and re-layouts: 300 us -> 16.7 us
  other arithmetic: 136 us -> 6.03 us
  blocking collectives: 88.1 us -> 16.1 us
  loops' own time: 32 us -> 0 us
  between operations: 16 us -> 0.96 us
    pallas_call x0 -> x21, Pallas kernels: none -> 676 us  [the longest x1 304 us: ring_all_reduce(): pl.pallas_call(ring_body, in_specs=[ANY, vmem], out_specs=[ANY, vmem], ou...]
    psum x1 -> x0, waiting for transfers between devices: 373 us -> none  [device_step(): summed = lax.psum(stacked, ('sp', 'dp'))]
    dot_general x71 -> x0, matrix products: 338 us -> none  [the longest x24 85.1 us: one_block(): jnp.einsum('hqk,khd->qhd', prob_bf, val_rows, preferred_element_type=jnp....]
    sub x16 -> x0, matrix products: 99.3 us -> none  [one_block(): prob_bf = jax.nn.softmax(scores, axis=-1).astype(jnp.bfloat16)]
    unnamed x213 -> x37, local copies, waits for them, and re-layouts: 97.2 us -> 8.47 us
    psum x1 -> x0, blocking collectives: 75.8 us -> none  [device_step(): summed = lax.psum(stacked, ('sp', 'dp'))]
    slice x39 -> x8, local copies, waits for them, and re-layouts: 70.3 us -> 5.68 us  [the longest x1 1.51 us: device_step(): kv_halo = halo_swap(qkv1[NHEAD:])]
    another operation x6 -> x0, other arithmetic: 58.7 us -> none  [device_step(): jnp.stack([first_grad, second_grad])]
  transfers between devices with their start and end apart: 8 -> 9, of which waited for: 5 -> 6; matrix products, arithmetic and copies ran while one was open for 7% -> 1% of each run, Pallas kernels for 0% -> 6%
where the time goes in v1:
time: 789 us; the launch traced here: 787 us
  Pallas kernels  676 us (86%)
  waiting for transfers between devices  43.9 us (6%)
  starting transfers between devices  28 us (4%)
  local copies, waits for them, and re-layouts  16.7 us (2%)
  blocking collectives  16.1 us (2%)
    pallas_call x1, Pallas kernels, ring_all_reduce(): pl.pallas_call(ring_body, in_specs=[ANY, vmem], out_specs=[ANY, vmem], ou...  304 us
    pallas_call x4, Pallas kernels, grad_call(): call(body, (steps,), [ANY] * len(shared) + in_specs, spec((rows, DM), lam...  58 us
    pallas_call x2, Pallas kernels, mlp_fwd(): call(mlp_fwd_body, (NFT,), [spec(ALLTOK), spec(o_t.shape), proj_spec(laye...  47.4 us
    pallas_call x2, Pallas kernels, mlp_bwd(): call(mlp_bwd_body, (NFT,), [spec(ALLTOK), spec(ALLTOK), spec((ONE, DM)),...  42.4 us
    all_to_all x3, waiting for transfers between devices, exchange(): return lax.all_to_all(arr, 'sp', ZERO, ZERO, tiled=True)  35.3 us
    pallas_call x2, Pallas kernels, qkv_bwd(): call(qkv_bwd_body, (PARTS,), [heads_spec(dest_major), table, table, weigh...  32.3 us
    pallas_call x1, Pallas kernels, attn0_bwd(): call(attn0_bwd_body, (QTILES,), [Q_SPEC, kv_spec(ONE), kv_spec(TWO), O_SP...  31.9 us
    pallas_call x1, Pallas kernels, attn0_fwd(): call(attn0_fwd_body, (QTILES,), [Q_SPEC, kv_spec(ONE), kv_spec(TWO), ROW_...  30.3 us
  transfers between devices with their start and end apart: 9, of which 6 were waited for; matrix products, arithmetic and copies ran while one was open for 1% of the time, Pallas kernels for 6%

profile of v1, /device:TPU:1, one launch (start us, length us, event | category | flops | bytes accessed | tf_op | source)
XLA Modules:
  0.0 787.5 jit_solution(17077504382800706117)
XLA Ops:
  3.9 11.2 %qkv_fwd.2 = (bf16[512,768]{1,0:T(8,128)(2,1)}, bf16[4,3,3,64,512]{4,3,2,1,0:T(8,128)(2,1)}, bf16[512,768]{1,0:T(8,128)(2,1)}) custom-call(bf16[512,768]{1,0:T(8,128)(2,1)} %x_ref.5, f32[1,768]{1,0:T(1,128)} %get-tuple-element.131.g_ref, bf16[2,768,2304]{2,1,0:T(8,128)(2,1)} %w_ref.7, f32[32,512]{1,0:T(8,128)} %get-tuple-element.136.cos_ref, ...), custom_call_target="tpu_custom_call" | custom-call | flops 1811939328 | bytes 8388608 | tf_op jit(solution)/shard_map/qkv_fwd/pallas_call | solution.py:187
  15.1 4.2 all-to-all-start
  20.2 27.8 %all-to-all-done.q_ref.k_ref.v_ref = bf16[4,3,3,64,512]{4,3,2,1,0:T(8,128)(2,1)S(1)} async-done(((bf16[4,3,3,64,512]{4,3,2,1,0:T(8,128)(2,1)}), bf16[4,3,3,64,512]{4,3,2,1,0:T(8,128)(2,1)S(1)}, u32[]{:S(2)}, u32[]{:S(2)}) %all-to-all-start) | async-done | bytes 2359328 | tf_op jit(solution)/shard_map/all_to_all | solution.py:990
  49.4 30.3 %attn0_fwd.1 = (bf16[4,3,64,512]{3,2,1,0:T(8,128)(2,1)}, f32[8,2048]{1,0:T(8,128)}) custom-call(s32[8]{0:T(128)} %get-tuple-element.141.lo_s, s32[8]{0:T(128)} %get-tuple-element.140.hi_s, bf16[4,3,3,64,512]{4,3,2,1,0:T(8,128)(2,1)} %copy-done.4, bf16[4,3,3,64,512]{4,3,2,1,0:T(8,128)(2,1)} %copy-done.4, bf16[4,3,3,64,512]{4,3,2,1,0:T(8,128)(2,1)} %copy-done.4, ...), custom_call_target="tpu_custom_call" | custom-call | flops 3221225472 | bytes 6291456 | tf_op jit(solution)/shard_map/attn0_fwd/pallas_call | solution.py:256
  79.8 3.5 all-to-all-start.1
  83.9 7.5 all-to-all-done.1.o_ref
  92.3 27.1 %mlp_fwd.2 = (bf16[512,768]{1,0:T(8,128)(2,1)}, bf16[512,768]{1,0:T(8,128)(2,1)}, bf16[2,512,3072]{2,1,0:T(8,128)(2,1)}, bf16[512,3072]{1,0:T(8,128)(2,1)}, bf16...) custom-call(bf16[512,768]{1,0:T(8,128)(2,1)} %x_ref.5, ...), custom_call_target="tpu_custom_call" | custom-call | flops 7851737088 | bytes 27262976 | tf_op jit(solution)/shard_map/mlp_fwd/pallas_call | solution.py:497
  119.3 10.1 %qkv_fwd.3 = (bf16[512,768]{1,0:T(8,128)(2,1)}, bf16[3,3,4,64,512]{4,3,2,1,0:T(8,128)(2,1)}, bf16[512,768]{1,0:T(8,128)(2,1)}) custom-call(bf16[512,768]{1,0:T(8,128)(2,1)} %get-tuple-element.63.x_ref, f32[1,768]{1,0:T(1,128)} %get-tuple-element.130.g_ref, bf16[2,768,2304]{2,1,0:T(8,128)(2,1)} %w_ref.7, f32[32,512]{1,0:T(8,128)} %get-tuple-element.133.cos_ref, ...), custom_call_target="tpu_custom_call" | custom-call | flops 1811939328 | bytes 8388608 | tf_op jit(solution)/shard_map/qkv_fwd/pallas_call | solution.py:187
  132.5 4.2 collective-permute-start
  138.7 4.8 collective-permute-done.1.kr_ref.vr_ref
  145.1 18.2 %attn1_fwd.1 = (bf16[12,64,512]{2,1,0:T(8,128)(2,1)}, f32[12,1,512]{2,1,0:T(1,128)}) custom-call(bf16[36,64,512]{2,1,0:T(8,128)(2,1)} %bitcast.14, bf16[36,64,512]{2,1,0:T(8,128)(2,1)} %bitcast.15, bf16[36,64,512]{2,1,0:T(8,128)(2,1)} %bitcast.16, bf16[24,64,128]{2,1,0:T(8,128)(2,1)} %copy-done.2, bf16[24,64,128]{2,1,0:T(8,128)(2,1)} %copy-done.2, ...), custom_call_target="tpu_custom_call" | custom-call | flops 603979776 | bytes 4194304 | tf_op jit(solution)/shard_map/attn1_fwd/pallas_call | solution.py:364
  164.1 20.4 %mlp_fwd.3 = (bf16[512,768]{1,0:T(8,128)(2,1)}, bf16[512,768]{1,0:T(8,128)(2,1)}, bf16[2,512,3072]{2,1,0:T(8,128)(2,1)}, bf16[512,3072]{1,0:T(8,128)(2,1)}, bf16...) custom-call(bf16[512,768]{1,0:T(8,128)(2,1)} %get-tuple-element.63.x, ...), custom_call_target="tpu_custom_call" | custom-call | flops 7851737088 | bytes 27262976 | tf_op jit(solution)/shard_map/mlp_fwd/pallas_call | solution.py:497
  184.5 21.2 %mlp_bwd.2 = (bf16[2,512,3072]{2,1,0:T(8,128)(2,1)}, bf16[512,768]{1,0:T(8,128)(2,1)}, f32[1,768]{1,0:T(1,128)}, bf16[12,64,512]{2,1,0:T(8,128)(2,1)}, f32[16,51...) custom-call(bf16[512,768]{1,0:T(8,128)(2,1)} %refs_2_.1, ...), custom_call_target="tpu_custom_call" | custom-call | flops 7851737088 | bytes 31457280 | tf_op jit(solution)/shard_map/mlp_bwd/pallas_call | solution.py:570
  208.2 4.8 collective-permute-start.2
  213.7 3.3 collective-permute-start.4
  218.6 2.8 collective-permute-done.4
  225.1 21.9 %attn1_bwd.1 = bf16[3,12,64,512]{3,2,1,0:T(8,128)(2,1)} custom-call(bf16[36,64,512]{2,1,0:T(8,128)(2,1)} %bitcast.17, bf16[36,64,512]{2,1,0:T(8,128)(2,1)} %bitcast.18, bf16[36,64,512]{2,1,0:T(8,128)(2,1)} %bitcast.19, bf16[12,64,512]{2,1,0:T(8,128)(2,1)} %get-tuple-element.70.do_ref, bf16[24,64,128]{2,1,0:T(8,128)(2,1)} %copy-done.2, ...), custom_call_target="tpu_custom_call" | custom-call | flops 1509949440 | bytes 8388608 | tf_op jit(solution)/shard_map/attn1_bwd/pallas_call | solution.py:407
  247.0 13.9 %qkv_bwd.2 = (bf16[2,1152,512]{2,1,0:T(8,128)(2,1)}, bf16[512,768]{1,0:T(8,128)(2,1)}, f32[1,768]{1,0:T(1,128)}, bf16[1152,512]{1,0:T(8,128)(2,1)}) custom-call(bf16[3,3,4,64,512]{4,3,2,1,0:T(8,128)(2,1)} %bitcast.20, f32[32,512]{1,0:T(8,128)} %get-tuple-element.133.cos_ref, f32[32,512]{1,0:T(8,128)} %get-tuple-element.132.sin_ref, ...), custom_call_target="tpu_custom_call" | custom-call | flops 1811939328 | bytes 10485760 | tf_op jit(solution)/shard_map/qkv_bwd/pallas_call | solution.py:631
  260.9 21.2 %mlp_bwd.3 = (bf16[2,512,3072]{2,1,0:T(8,128)(2,1)}, bf16[512,768]{1,0:T(8,128)(2,1)}, f32[1,768]{1,0:T(1,128)}, bf16[4,3,64,512]{3,2,1,0:T(8,128)(2,1)}, f32[16...) custom-call(bf16[512,768]{1,0:T(8,128)(2,1)} %get-tuple-element.74.dy_ref.refs_3_,, ...), custom_call_target="tpu_custom_call" | custom-call | flops 7851737088 | bytes 31457280 | tf_op jit(solution)/shard_map/mlp_bwd/pallas_call | solution.py:570
  282.1 16.1 %all_to_all.20.do_ref = bf16[4,3,64,512]{3,2,1,0:T(8,128)(2,1)} all-to-all(bf16[4,3,64,512]{3,2,1,0:T(8,128)(2,1)} %get-tuple-element.78), channel_id=1, replica_groups=mesh['sp'=4,'dp'=32] {'sp'}, dimensions={0} | all-to-all | bytes 1572864 | tf_op jit(solution)/shard_map/all_to_all | solution.py:990
  298.2 31.9 %attn0_bwd.1 = bf16[4,3,3,64,512]{4,3,2,1,0:T(8,128)(2,1)} custom-call(s32[8]{0:T(128)} %get-tuple-element.141.lo_s, s32[8]{0:T(128)} %get-tuple-element.140.hi_s, bf16[4,3,3,64,512]{4,3,2,1,0:T(8,128)(2,1)} %copy-done.4, bf16[4,3,3,64,512]{4,3,2,1,0:T(8,128)(2,1)} %copy-done.4, bf16[4,3,3,64,512]{4,3,2,1,0:T(8,128)(2,1)} %copy-done.4, ...), custom_call_target="tpu_custom_call" | custom-call | flops 8053063680 | bytes 12582912 | tf_op jit(solution)/shard_map/attn0_bwd/pallas_call | solution.py:313
  330.1 3.9 all-to-all-start.3
  334.0 21.7 %grad_mlp_body.2.refs_0_ = f32[12288,768]{1,0:T(8,128)} custom-call(s32[1]{0:T(128)} %bitcast.8.core_s, bf16[512,3072]{1,0:T(8,128)(2,1)} %get-tuple-element.82.refs_0_, bf16[3,512,512]{2,1,0:T(8,128)(2,1)} %get-tuple-element.83.refs_1_, bf16[512,768]{1,0:T(8,128)(2,1)} %refs_2_.1, bf16[512,768]{1,0:T(8,128)(2,1)} %get-tuple-element.84.refs_3_, ...), custom_call_target="tpu_custom_call" | custom-call | flops 7247757312 | bytes 20971520 | tf_op jit(solution)/shard_map/grad_mlp_body/pallas_call | solution.py:673
  355.6 7.4 grad_att_body.2.refs_0_
  363.0 21.6 %grad_mlp_body.3.refs_0_ = f32[12288,768]{1,0:T(8,128)} custom-call(s32[1]{0:T(128)} %bitcast.8.core_s, f32[12288,768]{1,0:T(8,128)} %grad_att_body.2.refs_0_, bf16[512,3072]{1,0:T(8,128)(2,1)} %get-tuple-element.95.refs_1_, bf16[3,512,512]{2,1,0:T(8,128)(2,1)} %get-tuple-element.96.refs_2_, ...), custom_call_target="tpu_custom_call", output_to_operand_aliasing={{}: (1, {})} | custom-call | flops 7247757312 | bytes 20971520 | tf_op jit(solution)/shard_map/grad_mlp_body/pallas_call | solution.py:673
  386.1 18.4 %qkv_bwd.3 = (bf16[2,1152,512]{2,1,0:T(8,128)(2,1)}, bf16[512,768]{1,0:T(8,128)(2,1)}, f32[1,768]{1,0:T(1,128)}, bf16[1152,512]{1,0:T(8,128)(2,1)}) custom-call(bf16[4,3,3,64,512]{4,3,2,1,0:T(8,128)(2,1)} %copy-done, f32[32,512]{1,0:T(8,128)} %get-tuple-element.136.cos_ref, f32[32,512]{1,0:T(8,128)} %get-tuple-element.137.sin_ref, ...), custom_call_target="tpu_custom_call" | custom-call | flops 1811939328 | bytes 10485760 | tf_op jit(solution)/shard_map/qkv_bwd/pallas_call | solution.py:631
  405.8 7.3 grad_att_body.3.g_ref
  413.2 303.8 %ring_all_reduce.1 = (f32[2,12288,768]{2,1,0:T(8,128)}, f32[8,768]{1,0:T(8,128)}) custom-call(f32[12288,768]{1,0:T(8,128)} %grad_att_body.3.g_ref, f32[8,768]{1,0:T(8,128)} %concatenate.15.ln_ref), custom_call_target="tpu_custom_call" | custom-call | tf_op jit(solution)/shard_map/ring_all_reduce/pallas_call | solution.py:921
  717.0 5.1 shard_map.162
  722.0 18.4 %shard_map.161 = f32[2,768,2304]{2,1,0:T(8,128)} custom-call(f32[2,12288,768]{2,1,0:T(8,128)} %get-tuple-element.112.a_ref.b_ref.in_ref, f32[2,12288,768]{2,1,0:T(8,128)} %get-tuple-element.112.a_ref.b_ref.in_ref), custom_call_target="tpu_custom_call" | custom-call | bytes 104857600 | tf_op jit(solution)/shard_map/pallas_call | solution.py:966
  740.4 15.0 %shard_map.164 = f32[2,3072,768]{2,1,0:T(8,128)} custom-call(f32[2,12288,768]{2,1,0:T(8,128)} %get-tuple-element.112.a_ref.b_ref.in_ref), custom_call_target="tpu_custom_call" | custom-call | bytes 104857600 | tf_op jit(solution)/shard_map/pallas_call | solution.py:955
  755.4 29.7 %shard_map.163 = f32[2,768,6144]{2,1,0:T(8,128)} custom-call(f32[2,12288,768]{2,1,0:T(8,128)} %get-tuple-element.112.a_ref.b_ref.in_ref), custom_call_target="tpu_custom_call" | custom-call | bytes 104857600 | tf_op jit(solution)/shard_map/pallas_call | solution.py:958
  (69 shorter events, 27.9 us)
Async XLA Ops:
  15.1 4.2 copy-start.16
  15.1 32.9 %all-to-all-start = ((bf16[4,3,3,64,512]{4,3,2,1,0:T(8,128)(2,1)}), bf16[4,3,3,64,512]{4,3,2,1,0:T(8,128)(2,1)S(1)}, u32[]{:S(2)}, u32[]{:S(2)}) async-start(bf16[4,3,3,64,512]{4,3,2,1,0:T(8,128)(2,1)} %get-tuple-element.61), calls=%async_computation | async-start | bytes 4718592 | tf_op jit(solution)/shard_map/all_to_all | solution.py:990
  19.4 28.6 %copy-start.9 = (s32[2048]{0:T(1024)}, s32[2048]{0:T(1024)S(1)}, u32[]{:S(2)}) copy-start(s32[2048]{0:T(1024)S(1)} %get-tuple-element.116) | copy-start | bytes 24580
  19.4 28.6 %copy-start.10 = (s32[2048]{0:T(1024)}, s32[2048]{0:T(1024)S(1)}, u32[]{:S(2)}) copy-start(s32[2048]{0:T(1024)S(1)} %get-tuple-element.117) | copy-start | bytes 24580
  48.0 1.4 copy-start.4
  49.4 33.9 %copy-start.12 = (f32[2,768]{1,0:T(2,128)S(1)}, f32[2,768]{1,0:T(2,128)}, u32[]{:S(2)}) copy-start(f32[2,768]{1,0:T(2,128)} %param.18) | copy-start | bytes 18436
  79.8 11.6 %all-to-all-start.1 = ((bf16[4,3,64,512]{3,2,1,0:T(8,128)(2,1)}), bf16[4,3,64,512]{3,2,1,0:T(8,128)(2,1)S(1)}, u32[]{:S(2)}, u32[]{:S(2)}) async-start(bf16[4,3,64,512]{3,2,1,0:T(8,128)(2,1)} %get-tuple-element.62.o_ref), calls=%async_computation.1 | async-start | bytes 1572864 | tf_op jit(solution)/shard_map/all_to_all | solution.py:990
  91.4 0.9 copy-start.3
  131.2 12.3 %collective-permute-start.1 = (bf16[24,64,128]{2,1,0:T(8,128)(2,1)S(1)}, bf16[24,64,128]{2,1,0:T(8,128)(2,1)S(1)}, u32[]{:S(2)}, u32[]{:S(2)}) collective-permute-start(bf16[24,64,128]{2,1,0:T(8,128)(2,1)S(1)} %get-tuple-element.120), channel_id=1, source_target_pairs={{32,0},{64,32},{96,64},{33,1},{65,33},{97,65},{34,2},{66,34},{98,6... | collective-permute-start | bytes 1179656 | tf_op jit(solution)/shard_map/ppermute | solution.py:986
  132.5 11.8 %collective-permute-start = (bf16[24,64,128]{2,1,0:T(8,128)(2,1)S(1)}, bf16[24,64,128]{2,1,0:T(8,128)(2,1)S(1)}, u32[]{:S(2)}, u32[]{:S(2)}) collective-permute-start(bf16[24,64,128]{2,1,0:T(8,128)(2,1)S(1)} %get-tuple-element.121), channel_id=1, source_target_pairs={{0,32},{32,64},{64,96},{1,33},{33,65},{65,97},{2,34},{34,66},{66,9... | collective-permute-start | bytes 1179656 | tf_op jit(solution)/shard_map/ppermute | solution.py:985
  143.5 0.9 copy-start.1
  144.4 0.7 copy-start.2
  206.9 16.7 %collective-permute-start.3 = (bf16[24,64,128]{2,1,0:T(8,128)(2,1)S(1)}, bf16[24,64,128]{2,1,0:T(8,128)(2,1)S(1)}, u32[]{:S(2)}, u32[]{:S(2)}) collective-permute-start(bf16[24,64,128]{2,1,0:T(8,128)(2,1)S(1)} %get-tuple-element.118), channel_id=1, source_target_pairs={{32,0},{64,32},{96,64},{33,1},{65,33},{97,65},{34,2},{66,34},{98,6... | collective-permute-start | bytes 1179656 | tf_op jit(solution)/shard_map/ppermute | solution.py:986
  208.2 15.4 %collective-permute-start.2 = (bf16[24,64,128]{2,1,0:T(8,128)(2,1)S(1)}, bf16[24,64,128]{2,1,0:T(8,128)(2,1)S(1)}, u32[]{:S(2)}, u32[]{:S(2)}) collective-permute-start(bf16[24,64,128]{2,1,0:T(8,128)(2,1)S(1)} %get-tuple-element.119), channel_id=1, source_target_pairs={{0,32},{32,64},{64,96},{1,33},{33,65},{65,97},{2,34},{34,66},{66,9... | collective-permute-start | bytes 1179656 | tf_op jit(solution)/shard_map/ppermute | solution.py:985
  213.7 7.6 collective-permute-start.4
  217.0 4.4 collective-permute-start.5
  223.5 0.8 copy-start.5
  224.3 0.7 copy-start.6
  330.1 54.6 %all-to-all-start.3 = ((bf16[4,3,3,64,512]{4,3,2,1,0:T(8,128)(2,1)}), bf16[4,3,3,64,512]{4,3,2,1,0:T(8,128)(2,1)S(1)}, u32[]{:S(2)}, u32[]{:S(2)}) async-start(bf16[4,3,3,64,512]{4,3,2,1,0:T(8,128)(2,1)} %attn0_bwd.1), calls=%async_computation.3 | async-start | bytes 4718592 | tf_op jit(solution)/shard_map/all_to_all | solution.py:990
  384.6 1.4 copy-start
  386.0 18.5 %copy-start.13 = (f32[1,768]{1,0:T(1,128)S(1)}, f32[1,768]{1,0:T(1,128)}, u32[]{:S(2)}) copy-start(f32[1,768]{1,0:T(1,128)} %get-tuple-element.111) | copy-start | bytes 9220
  386.1 18.5 %copy-start.14 = (f32[1,768]{1,0:T(1,128)S(1)}, f32[1,768]{1,0:T(1,128)}, u32[]{:S(2)}) copy-start(f32[1,768]{1,0:T(1,128)} %get-tuple-element.109) | copy-start | bytes 9220
  386.1 18.5 %copy-start.15 = (f32[1,768]{1,0:T(1,128)S(1)}, f32[1,768]{1,0:T(1,128)}, u32[]{:S(2)}) copy-start(f32[1,768]{1,0:T(1,128)} %get-tuple-element.110) | copy-start | bytes 9220
  755.4 29.7 %copy-start.11 = (f32[8,768]{1,0:T(8,128)S(1)}, f32[8,768]{1,0:T(8,128)}, u32[]{:S(2)}) copy-start(f32[8,768]{1,0:T(8,128)} %get-tuple-element.113) | copy-start | bytes 73732
  755.4 30.3 %copy-start.7 = (bf16[512,768]{1,0:T(8,128)(2,1)S(1)}, bf16[512,768]{1,0:T(8,128)(2,1)}, u32[]{:S(2)}) copy-start(bf16[512,768]{1,0:T(8,128)(2,1)} %get-tuple-element.152) | copy-start | bytes 2359300
  755.4 31.2 %copy-start.8 = (bf16[512,768]{1,0:T(8,128)(2,1)S(1)}, bf16[512,768]{1,0:T(8,128)(2,1)}, u32[]{:S(2)}) copy-start(bf16[512,768]{1,0:T(8,128)(2,1)} %get-tuple-element.153) | copy-start | bytes 2359300

commit v2 on v1

--- a/solution.py
+++ b/solution.py
@@ -30,6 +30,7 @@
 QTILES = GRP // QT
 MIB = 1024 * 1024
 ALLTOK = (TOK, DM)
+PROJ = DM // 2
 ANY = pl.BlockSpec(memory_space=pl.ANY)
 DMA = pltpu.SemaphoreType.DMA
 MESH = pl.DeviceIdType.MESH
@@ -122,26 +123,18 @@
     return (a.astype(F32) + b.astype(F32)).astype(BF)
 
 
-PARTS = 9
-ROPED = 6
-
-
-def part_of(s, *_):
-    return s // THREE
-
-
-def slot_of(s, *_):
-    return s % THREE
-
-
-def head_rows(ref, head):
-    return ref.at[head, ZERO, ZERO] if ref.shape[ZERO] == FOUR else ref.at[ZERO, ZERO, head]
+RB = 256
+CHUNKS = range(DM // RB)
+
+
+def head_rows(ref, chunk, head):
+    return ref.at[head, ZERO, chunk] if ref.shape[ZERO] == FOUR else ref.at[ZERO, chunk, head]
 
 
 def heads_spec(dest_major):
     if dest_major:
-        return spec((FOUR, ONE, ONE, HEAD, TOK), ZERO, part_of, slot_of, ZERO, ZERO)
-    return spec((ONE, ONE, FOUR, HEAD, TOK), part_of, slot_of, ZERO, ZERO, ZERO)
+        return spec((FOUR, ONE, THREE, HEAD, TOK), ZERO, step_of, ZERO, ZERO, ZERO)
+    return spec((ONE, THREE, FOUR, HEAD, TOK), step_of, ZERO, ZERO, ZERO, ZERO)
 
 
 def weight_cols(layer, width, first=ZERO):
@@ -159,25 +152,27 @@
         meet_partner(partner)
         swap.start()
 
-    t_rows = mm(h_ref[...], w_ref[...]).astype(BF).astype(F32).T
-
-    @pl.when(step < ROPED)
+    def product(chunk):
+        return mm(h_ref[...], w_ref[:, RB * chunk:RB * chunk + RB]).astype(BF).astype(F32).T
+
+    @pl.when(step < TWO)
     def _():
         cos, sin = cos_ref[...], sin_ref[...]
-        for head in range(FOUR):
-            at = HEAD * head
-            a, b = t_rows[at:at + HALF], t_rows[at + HALF:at + HEAD]
-            out = head_rows(out_ref, head)
-            out[:HALF] = (a * cos - b * sin).astype(BF)
-            out[HALF:] = (b * cos + a * sin).astype(BF)
-
-    @pl.when(step >= ROPED)
-    def _():
-        for head in range(FOUR):
-            head_rows(out_ref, head)[...] = t_rows[HEAD * head:HEAD * head + HEAD].astype(BF)
-
-    @pl.when(step == PARTS - ONE)
-    def _():
+        for chunk in CHUNKS:
+            t_rows = product(chunk)
+            for head in range(FOUR):
+                at = HEAD * head
+                a, b = t_rows[at:at + HALF], t_rows[at + HALF:at + HEAD]
+                out = head_rows(out_ref, chunk, head)
+                out[:HALF] = (a * cos - b * sin).astype(BF)
+                out[HALF:] = (b * cos + a * sin).astype(BF)
+
+    @pl.when(step == TWO)
+    def _():
+        for chunk in CHUNKS:
+            t_rows = product(chunk).astype(BF)
+            for head in range(FOUR):
+                head_rows(out_ref, chunk, head)[...] = t_rows[HEAD * head:HEAD * head + HEAD]
         swap.wait()
 
 
@@ -185,8 +180,8 @@
     oshape = (FOUR, THREE, THREE, HEAD, TOK) if dest_major else (THREE, THREE, FOUR, HEAD, TOK)
     table = spec((HALF, TOK))
     return call(
-        qkv_fwd_body, (PARTS,),
-        [spec(ALLTOK), spec((ONE, DM)), weight_cols(layer, QT), table, table],
+        qkv_fwd_body, (THREE,),
+        [spec(ALLTOK), spec((ONE, DM)), weight_cols(layer, DM), table, table],
         [spec(ALLTOK), heads_spec(dest_major), ANY],
         [sds(ALLTOK, BF), sds(oshape, BF), sds(ALLTOK, BF)],
         scratch=[DMA, DMA],
@@ -323,16 +318,24 @@
 EXT = TOK + TWO * LANE
 
 
+HPS = 4
+HSTEPS = NHEAD // HPS
+
+
+def heads_of(width, part):
+    return spec((HPS, HEAD, width), lambda n: HSTEPS * part + n, ZERO, ZERO)
+
+
 def own_head(part):
-    return spec((ONE, HEAD, TOK), lambda n: NHEAD * part + n, ZERO, ZERO)
+    return heads_of(TOK, part)
 
 
 def halo_head(part):
-    return spec((ONE, HEAD, LANE), lambda n: NHEAD * part + n, ZERO, ZERO)
-
-
-def joined(left, mid, right):
-    return jnp.concatenate([left[ZERO], mid[ZERO], right[ZERO]], axis=ONE)
+    return heads_of(LANE, part)
+
+
+def joined(left, mid, right, h):
+    return jnp.concatenate([left[h], mid[h], right[h]], axis=ONE)
 
 
 def blocks(first, last):
@@ -345,27 +348,36 @@
     return (io >= lo_ref[:, cols]) & (io < hi_ref[:, cols])
 
 
+def every_head(fn):
+    def body(h, c):
+        fn(h)
+        return c
+    lax.fori_loop(ZERO, HPS, body, ZERO)
+
+
 def attn1_fwd_body(q_ref, k_ref, v_ref, kl_ref, vl_ref, kr_ref, vr_ref, lo_ref, hi_ref, o_ref, lse_ref):
-    q_t = q_ref[ZERO] * SCALE
-    k_t = joined(kl_ref, k_ref, kr_ref)
-    v_t = joined(vl_ref, v_ref, vr_ref)
-    for i in range(NBLK):
-        cols, wide = blocks(i, i + ONE), blocks(i, i + THREE)
-        s = jnp.where(in_bounds(lo_ref, hi_ref, i + ONE, i, i + THREE), mm_tn(k_t[:, wide], q_t[:, cols]), NEG)
-        m = jnp.max(s, axis=ZERO, keepdims=True)
-        e = jnp.exp(s - m)
-        l = jnp.sum(e, axis=ZERO, keepdims=True)
-        o_ref[ZERO, :, cols] = mm(v_t[:, wide], (e / l).astype(BF)).astype(BF)
-        lse_ref[ZERO, :, cols] = m + jnp.log(l)
+    def head(h):
+        q_t = q_ref[h] * SCALE
+        k_rows = joined(kl_ref, k_ref, kr_ref, h).T
+        v_t = joined(vl_ref, v_ref, vr_ref, h)
+        for i in range(NBLK):
+            cols, wide = blocks(i, i + ONE), blocks(i, i + THREE)
+            s = jnp.where(in_bounds(lo_ref, hi_ref, i + ONE, i, i + THREE), mm(k_rows[wide], q_t[:, cols]), NEG)
+            m = jnp.max(s, axis=ZERO, keepdims=True)
+            e = jnp.exp(s - m)
+            l = jnp.sum(e, axis=ZERO, keepdims=True)
+            o_ref[h, :, cols] = mm(v_t[:, wide], (e * (ONE / l)).astype(BF)).astype(BF)
+            lse_ref[h, :, cols] = m + jnp.log(l)
+    every_head(head)
 
 
 def attn1_fwd(qkv, left, right, lo, hi):
     bound = spec((ONE, EXT))
     return call(
-        attn1_fwd_body, (NHEAD,),
+        attn1_fwd_body, (HSTEPS,),
         [own_head(ZERO), own_head(ONE), own_head(TWO), halo_head(ZERO), halo_head(ONE), halo_head(ZERO), halo_head(ONE),
          bound, bound],
-        [own_head(ZERO), spec((ONE, ONE, TOK), step_of, ZERO, ZERO)],
+        [own_head(ZERO), spec((HPS, ONE, TOK), step_of, ZERO, ZERO)],
         [sds((NHEAD, HEAD, TOK), BF), sds((NHEAD, ONE, TOK), F32)],
         flops=NHEAD * FOUR * TOK * EXT * HALF, nbytes=FOUR * MIB, name="attn1_fwd",
     )(qkv, qkv, qkv, left, left, right, right, lo, hi)
@@ -373,53 +385,54 @@
 
 def attn1_bwd_body(q_ref, k_ref, v_ref, do_ref, kl_ref, vl_ref, kr_ref, vr_ref, ql_ref, dl_ref, qr_ref, dr_ref,
                    lse_ref, del_ref, lo_ref, hi_ref, out_ref):
-    q_t = joined(ql_ref, q_ref, qr_ref) * SCALE
-    do_t = joined(dl_ref, do_ref, dr_ref)
-    k_t = joined(kl_ref, k_ref, kr_ref)
-    v_t = joined(vl_ref, v_ref, vr_ref)
     last_own = NBLK + ONE
-    dk = [jnp.zeros((HEAD, LANE), F32) for _ in range(last_own)]
-    dv = [jnp.zeros((HEAD, LANE), F32) for _ in range(last_own)]
-    for e in range(NBLK + TWO):
-        mine = ONE <= e <= NBLK
-        first = e - ONE if mine else max(e - ONE, ONE)
-        last = e + TWO if mine else min(e + TWO, last_own)
-        cols, wide = blocks(e, e + ONE), blocks(first, last)
-        ok = in_bounds(lo_ref, hi_ref, e, first, last)
-        p = jnp.exp(jnp.where(ok, mm_tn(k_t[:, wide], q_t[:, cols]) - lse_ref[ZERO, :, cols], NEG))
-        ds = jnp.where(ok, p * (mm_tn(v_t[:, wide], do_t[:, cols]) - del_ref[ZERO, :, cols]), F32(ZERO)).astype(BF)
-        p_bf = p.astype(BF)
-        if mine:
-            out_ref[ZERO, ZERO, :, blocks(e - ONE, e)] = (mm(k_t[:, wide], ds) * SCALE).astype(BF)
-        for kb in range(max(first, ONE), min(last, last_own)):
-            rows = blocks(kb - first, kb - first + ONE)
-            dv[kb] += mm_nt(do_t[:, cols], p_bf[rows])
-            dk[kb] += mm_nt(q_t[:, cols], ds[rows])
-    for kb in range(ONE, last_own):
-        out_ref[ONE, ZERO, :, blocks(kb - ONE, kb)] = dk[kb].astype(BF)
-        out_ref[TWO, ZERO, :, blocks(kb - ONE, kb)] = dv[kb].astype(BF)
+
+    def head(h):
+        q_t = joined(ql_ref, q_ref, qr_ref, h) * SCALE
+        do_t = joined(dl_ref, do_ref, dr_ref, h)
+        k_t = joined(kl_ref, k_ref, kr_ref, h)
+        k_rows, v_rows = k_t.T, joined(vl_ref, v_ref, vr_ref, h).T
+        dk = [jnp.zeros((HEAD, LANE), F32) for _ in range(last_own)]
+        dv = [jnp.zeros((HEAD, LANE), F32) for _ in range(last_own)]
+        for e in range(NBLK + TWO):
+            mine = ONE <= e <= NBLK
+            first = e - ONE if mine else max(e - ONE, ONE)
+            last = e + TWO if mine else min(e + TWO, last_own)
+            cols, wide = blocks(e, e + ONE), blocks(first, last)
+            ok = in_bounds(lo_ref, hi_ref, e, first, last)
+            p = jnp.exp(jnp.where(ok, mm(k_rows[wide], q_t[:, cols]) - lse_ref[h, :, cols], NEG))
+            ds = (p * (mm(v_rows[wide], do_t[:, cols]) - del_ref[h, :, cols])).astype(BF)
+            p_bf = p.astype(BF)
+            if mine:
+                out_ref[ZERO, h, :, blocks(e - ONE, e)] = (mm(k_t[:, wide], ds) * SCALE).astype(BF)
+            for kb in range(max(first, ONE), min(last, last_own)):
+                rows = blocks(kb - first, kb - first + ONE)
+                dv[kb] += mm_nt(do_t[:, cols], p_bf[rows])
+                dk[kb] += mm_nt(q_t[:, cols], ds[rows])
+        for kb in range(ONE, last_own):
+            out_ref[ONE, h, :, blocks(kb - ONE, kb)] = dk[kb].astype(BF)
+            out_ref[TWO, h, :, blocks(kb - ONE, kb)] = dv[kb].astype(BF)
+    every_head(head)
 
 
 def attn1_bwd(qkv, do_t, left, right, dleft, dright, lse_x, del_x, lo, hi):
-    stat = spec((ONE, ONE, EXT), step_of, ZERO, ZERO)
+    stat = spec((HPS, ONE, EXT), step_of, ZERO, ZERO)
     bound = spec((ONE, EXT))
     pair = [halo_head(ZERO), halo_head(ONE)]
     return call(
-        attn1_bwd_body, (NHEAD,),
+        attn1_bwd_body, (HSTEPS,),
         [own_head(ZERO), own_head(ONE), own_head(TWO), own_head(ZERO)] + pair * FOUR + [stat, stat, bound, bound],
-        spec((THREE, ONE, HEAD, TOK), ZERO, step_of, ZERO, ZERO),
+        spec((THREE, HPS, HEAD, TOK), ZERO, step_of, ZERO, ZERO),
         sds((THREE, NHEAD, HEAD, TOK), BF),
         flops=NHEAD * 10 * TOK * EXT * HALF, nbytes=8 * MIB, name="attn1_bwd",
     )(qkv, qkv, qkv, do_t, left, left, right, right, dleft, dleft, dright, dright, lse_x, del_x, lo, hi)
 
 
-RB = 256
 ROWBLK = [slice(r, r + RB) for r in range(ZERO, TOK, RB)]
 HALFT = NFT // TWO
 SQRT_HALF = math.sqrt(SCALE * FOUR)
 PDF_SCALE = SQRT_HALF / math.sqrt(math.pi)
-UBLK = (TWO, TOK, FT)
-U_SPEC = spec(UBLK, ZERO, ZERO, step_of)
+STATS = 16
 
 
 def normal_cdf(a):
@@ -435,278 +448,286 @@
     return ref.at[pl.ds(pl.multiple_of(which * n, n), n)]
 
 
-def mlp_fwd_body(x_ref, o_ref, wp_ref, g_ref, wa_ref, wb_ref, wo_ref, x1_ref, h_ref, u_ref, m_ref, y_ref, of_ref,
-                 mr_ref, hr_ref, or_ref, acc, m_s, ssem, rsem):
+def col_tile(ref, n):
+    return ref.at[:, pl.ds(pl.multiple_of(n * FT, FT), FT)]
+
+
+class Refs:
+    def __init__(self, names, refs):
+        self.__dict__.update(zip(names, refs))
+
+
+class Swaps:
+    def __init__(self, r):
+        self.r, self.waits, self.n = r, [], ZERO
+        self.core, self.partner = core_and_partner()
+        self.other = ONE - self.core
+
+    def remote(self, src, dst):
+        cp = to_partner(self.partner, src, dst, self.r.ssem.at[self.n], self.r.rsem.at[self.n])
+        return self.later(cp)
+
+    def local(self, src, dst):
+        return self.later(pltpu.make_async_copy(src, dst, self.r.lsem.at[self.n]))
+
+    def later(self, cp):
+        self.n += ONE
+        self.waits.append(cp)
+        return cp
+
+    def wait(self):
+        for cp in self.waits:
+            cp.wait()
+
+
+def mlp_body(*refs, names, fwd, bwd):
+    r = Refs(names, refs)
+    step = pl.program_id(ZERO)
+    sw = Swaps(r)
+    start, spread = [], []
+    if fwd:
+        start = [sw.remote(r.h, r.h_r), sw.remote(half_rows(r.of, sw.other), r.of_r),
+                 sw.local(half_rows(r.of, sw.core), r.of_m)]
+        m_out = [(sw.remote(r.m_s.at[HALFT * sw.other + n], col_tile(r.m_r, n)),
+                  sw.local(r.m_s.at[HALFT * sw.core + n], col_tile(r.m_m, n))) for n in range(HALFT)]
+    if bwd:
+        start.append(sw.remote(r.dy, r.dy_r))
+        dmid_out = sw.remote(r.dmid, r.dmid_r)
+        du_out = [(sw.remote(r.du_s.at[n, sw.other], col_tile(r.du_r, n)),
+                   sw.local(r.du_s.at[n, sw.core], col_tile(r.du_m, n))) for n in range(NFT)]
+
+    @pl.when(step == ZERO)
+    def _():
+        if fwd:
+            for n in range(NHEAD):
+                r.of[HEAD * n:HEAD * n + HEAD, :] = att_block(r.o, n)[...]
+            x1 = (r.x[...].astype(F32) + mm_tn(r.of[...], r.wp[...])).astype(BF)
+            r.x1[...] = x1
+            r.h[...] = norm_rows(x1, r.g[...])
+            r.acc[...] = x1.astype(F32)
+        if bwd:
+            r.dacc[...] = jnp.zeros(r.dacc.shape, F32)
+        meet_partner(sw.partner)
+        for cp in start:
+            cp.start()
+
+    for rows in ROWBLK:
+        if fwd:
+            ua = mm(r.h[rows], r.wa[...]).astype(BF)
+            ub = mm(r.h[rows], r.wb[...]).astype(BF)
+            if not bwd:
+                r.u[ZERO, rows] = ua
+                r.u[ONE, rows] = ub
+        else:
+            ua, ub = r.u[ZERO, rows], r.u[ONE, rows]
+        a, b = ua.astype(F32), ub.astype(F32)
+        cdf = normal_cdf(a)
+        gate = a * cdf
+        if fwd:
+            m = (gate * b).astype(BF)
+            r.m_s[step, rows] = m
+            r.acc[rows] += mm(m, r.wo[...])
+        if bwd:
+            dm = mm_nt(r.dy[rows], r.wo[...]).astype(BF).astype(F32)
+            pdf = jnp.exp(a * a * (SCALE * FOUR - ONE)) * PDF_SCALE
+            db = (dm * gate).astype(BF)
+            da = (dm * b * (cdf + a * pdf)).astype(BF)
+            r.du_s[step, ZERO, rows] = da
+            r.du_s[step, ONE, rows] = db
+            r.dacc[rows] += mm_nt(da, r.wa[...]) + mm_nt(db, r.wb[...])
+
+    for n in range(NFT):
+        @pl.when(step == n)
+        def _(n=n):
+            if fwd:
+                there, here = m_out[n % HALFT]
+
+                @pl.when(sw.core == n // HALFT)
+                def _():
+                    here.start()
+
+                @pl.when(sw.other == n // HALFT)
+                def _():
+                    there.start()
+            if bwd:
+                for cp in du_out[n]:
+                    cp.start()
+
+    @pl.when(step == NFT - ONE)
+    def _():
+        if fwd:
+            r.y[...] = r.acc[...].astype(BF)
+        if bwd:
+            d_ln, gg = norm_rows_grad(r.x1[...], r.g[...], r.dacc[...].astype(BF))
+            r.gg[...] = gg
+            d_mid = add_bf(r.dy[...], d_ln)
+            r.dmid[...] = d_mid
+            dmid_out.start()
+            d_att = mm_nt(r.wp[...], d_mid).astype(BF)
+            for n in range(NHEAD):
+                rows = slice(HEAD * n, HEAD * n + HEAD)
+                blk = d_att[rows]
+                att_block(r.d_o, n)[...] = blk
+                if fwd:
+                    r.delta[n:n + ONE, :] = jnp.sum(blk.astype(F32) * r.of[rows].astype(F32), axis=ZERO, keepdims=True)
+            if fwd:
+                r.delta[NHEAD:, :] = jnp.zeros((STATS - NHEAD, TOK), F32)
+        sw.wait()
+
+
+def mlp_call(layer, cid, fwd, bwd, w_proj, gain, w_in, w_out, x=None, o_t=None, dy=None, x1=None, u=None, oshape=None):
+    toks, tok_spec, vec = sds(ALLTOK, BF), spec(ALLTOK), spec((ONE, DM))
+    u_spec = spec((TWO, TOK, FT), ZERO, ZERO, step_of)
+    half_o = sds((DM // TWO, TOK), BF)
+    half_m, half_u = sds((TOK, FF // TWO), BF), sds((TOK, FF), BF)
+    ins = [('wp', w_proj, spec((None, DM, DM), layer, ZERO, ZERO)), ('g', gain, vec),
+           ('wa', w_in, weight_cols(layer, FT)), ('wb', w_in, weight_cols(layer, FT, NFT)),
+           ('wo', w_out, spec((None, FT, DM), layer, step_of, ZERO))]
+    outs, scratch = [], []
+    if fwd:
+        ins += [('x', x, tok_spec), ('o', o_t, spec(o_t.shape))]
+        outs += [('y', toks, tok_spec), ('h', toks, tok_spec), ('h_r', toks, ANY), ('of_m', half_o, ANY), ('of_r', half_o, ANY),
+                 ('m_m', half_m, ANY), ('m_r', half_m, ANY)]
+        scratch += [('acc', pltpu.VMEM(ALLTOK, F32)), ('of', pltpu.VMEM((DM, TOK), BF)), ('m_s', pltpu.VMEM((NFT, TOK, FT), BF))]
+    if fwd and not bwd:
+        outs += [('x1', toks, tok_spec), ('u', sds((TWO, TOK, FF), BF), u_spec)]
+    if bwd:
+        ins += [('dy', dy, tok_spec)]
+        outs += [('dmid', toks, tok_spec), ('gg', sds((ONE, DM), F32), vec), ('d_o', sds(oshape, BF), spec(oshape)),
+                 ('dy_r', toks, ANY), ('dmid_r', toks, ANY), ('du_m', half_u, ANY), ('du_r', half_u, ANY)]
+        scratch += [('dacc', pltpu.VMEM(ALLTOK, F32)), ('du_s', pltpu.VMEM((NFT, TWO, TOK, FT), BF))]
+    if fwd and bwd:
+        outs += [('delta', sds((STATS, TOK), F32), spec((STATS, TOK)))]
+        scratch += [('x1', pltpu.VMEM(ALLTOK, BF))]
+    if not fwd:
+        ins += [('x1', x1, tok_spec), ('u', u, u_spec)]
+    sems = DMA((TWO * NFT + 8 + NFT,))
+    scratch += [('ssem', sems), ('rsem', sems), ('lsem', sems)]
+    names = [n for n, *_ in ins + outs + scratch]
+    name = "mlp_" + "fwd" * fwd + "bwd" * bwd
+    got = call(
+        functools.partial(mlp_body, names=names, fwd=fwd, bwd=bwd), (NFT,),
+        [sp for *_, sp in ins], [sp for *_, sp in outs], [sh for _, sh, _ in outs], scratch=[sh for _, sh in scratch],
+        flops=TWO * TOK * DM * (DM + THREE * FF) * (fwd + bwd), nbytes=26 * MIB, name=name, cid=cid,
+    )(*[arr for _, arr, _ in ins])
+    return Refs([n for n, *_ in outs], got)
+
+
+def qkv_bwd_body(d_ref, cos_ref, sin_ref, w_ref, x_ref, g_ref, dmid_ref, dx_ref, gg_ref, dtm_ref, dtr_ref,
+                 acc, dt_s, dt_all, ssem, rsem, lsem):
     step = pl.program_id(ZERO)
     core, partner = core_and_partner()
-    other = ONE - core
-
-    def send(n, src, dst):
-        return to_partner(partner, src, dst, ssem.at[n], rsem.at[n])
-
-    small = [send(HALFT, h_ref, hr_ref), send(HALFT + ONE, half_rows(of_ref, other), or_ref)]
-
-    @pl.when(step == ZERO)
-    def _():
-        for n in range(NHEAD):
-            of_ref[HEAD * n:HEAD * n + HEAD, :] = att_block(o_ref, n)[...]
-        x1 = (x_ref[...].astype(F32) + mm_tn(of_ref[...], wp_ref[...])).astype(BF)
-        x1_ref[...] = x1
-        h_ref[...] = norm_rows(x1, g_ref[...])
-        acc[...] = x1.astype(F32)
-        meet_partner(partner)
-        for cp in small:
-            cp.start()
-
-    slot = lax.rem(step, HALFT)
-    for rows in ROWBLK:
-        ua = mm(h_ref[rows], wa_ref[...]).astype(BF)
-        ub = mm(h_ref[rows], wb_ref[...]).astype(BF)
-        u_ref[ZERO, rows] = ua
-        u_ref[ONE, rows] = ub
-        a = ua.astype(F32)
-        m = ((a * normal_cdf(a)) * ub.astype(F32)).astype(BF)
-        m_ref[rows] = m
-        acc[rows] += mm(m, wo_ref[...])
-
-    @pl.when(step // HALFT == other)
-    def _():
-        m_s[slot] = m_ref[...]
-        send(slot, m_s.at[slot], mr_ref.at[slot]).start()
-
-    @pl.when(step == NFT - ONE)
-    def _():
-        y_ref[...] = acc[...].astype(BF)
-        for n in range(HALFT):
-            send(n, m_s.at[n], mr_ref.at[n]).wait()
-        for cp in small:
-            cp.wait()
-
-
-def proj_spec(layer):
-    return spec((None, DM, DM), layer, ZERO, ZERO)
-
-
-def out_weight(layer):
-    return spec((None, FT, DM), layer, step_of, ZERO)
-
-
-def mlp_fwd(x, o_t, w_proj, gain, w_in, w_out, layer, cid):
-    half_m = (HALFT, TOK, FT)
-    toks = sds(ALLTOK, BF)
-    return call(
-        mlp_fwd_body, (NFT,),
-        [spec(ALLTOK), spec(o_t.shape), proj_spec(layer), spec((ONE, DM)),
-         weight_cols(layer, FT), weight_cols(layer, FT, NFT), out_weight(layer)],
-        [spec(ALLTOK), spec(ALLTOK), U_SPEC, spec((TOK, FT), ZERO, step_of), spec(ALLTOK), spec((DM, TOK)), ANY, ANY, ANY],
-        [toks, toks, sds((TWO, TOK, FF), BF), sds((TOK, FF), BF), toks, sds((DM, TOK), BF),
-         sds(half_m, BF), toks, sds((DM // TWO, TOK), BF)],
-        scratch=[pltpu.VMEM(ALLTOK, F32), pltpu.VMEM(half_m, BF), DMA((HALFT + TWO,)), DMA((HALFT + TWO,))],
-        flops=TWO * TOK * DM * (DM + THREE * FF), nbytes=26 * MIB, name="mlp_fwd", cid=cid,
-    )(x, o_t, w_proj, gain, w_in, w_in, w_out)
-
-
-STATS = 16
-
-
-def mlp_bwd_body(dy_ref, x1_ref, g_ref, wa_ref, wb_ref, wo_ref, u_ref, wp_ref, of_ref,
-                 du_ref, dmid_ref, gg_ref, dot_ref, del_ref, dur_ref, dyr_ref, dmr_ref, acc, du_s, ssem, rsem):
-    step = pl.program_id(ZERO)
-    core, partner = core_and_partner()
-
-    def send(n, src, dst):
-        return to_partner(partner, src, dst, ssem.at[n], rsem.at[n])
-
-    def send_du(n):
-        return send(n, du_s.at[n], dur_ref.at[:, pl.ds(pl.multiple_of(n * FT, FT), FT)])
-
-    send_dy = send(NFT, dy_ref, dyr_ref)
-    send_dmid = send(NFT + ONE, dmid_ref, dmr_ref)
+
+    def dst(ref, n):
+        rows = PROJ
+        return ref.at[pl.ds(pl.multiple_of(n * rows, rows), rows)]
+
+    def copies(n):
+        return (to_partner(partner, dt_s.at[ONE - core, n], dst(dtr_ref, n), ssem.at[n], rsem.at[n]),
+                pltpu.make_async_copy(dt_s.at[core, n], dst(dtm_ref, n), lsem.at[n]))
 
     @pl.when(step == ZERO)
     def _():
         acc[...] = jnp.zeros(acc.shape, F32)
         meet_partner(partner)
-        send_dy.start()
-
-    for rows in ROWBLK:
-        dm = mm_nt(dy_ref[rows], wo_ref[...]).astype(BF).astype(F32)
-        a = u_ref[ZERO, rows].astype(F32)
-        b = u_ref[ONE, rows].astype(F32)
-        cdf = normal_cdf(a)
-        pdf = jnp.exp(a * a * (SCALE * FOUR - ONE)) * PDF_SCALE
-        db = (dm * (a * cdf)).astype(BF)
-        da = (dm * b * (cdf + a * pdf)).astype(BF)
-        du_ref[ZERO, rows] = da
-        du_ref[ONE, rows] = db
-        acc[rows] += mm_nt(da, wa_ref[...]) + mm_nt(db, wb_ref[...])
-
-    du_s[step] = du_ref[ONE - core]
-    send_du(step).start()
-
-    @pl.when(step == NFT - ONE)
-    def _():
-        d_ln, gg = norm_rows_grad(x1_ref[...], g_ref[...], acc[...].astype(BF))
-        gg_ref[...] = gg
-        d_mid = add_bf(dy_ref[...], d_ln)
-        dmid_ref[...] = d_mid
-        send_dmid.start()
-        d_att = mm_nt(wp_ref[...], d_mid).astype(BF)
-        for n in range(NHEAD):
-            rows = slice(HEAD * n, HEAD * n + HEAD)
-            blk = d_att[rows]
-            att_block(dot_ref, n)[...] = blk
-            del_ref[n:n + ONE, :] = jnp.sum(blk.astype(F32) * of_ref[rows].astype(F32), axis=ZERO, keepdims=True)
-        del_ref[NHEAD:, :] = jnp.zeros((STATS - NHEAD, TOK), F32)
-        for n in range(NFT):
-            send_du(n).wait()
-        send_dy.wait()
-        send_dmid.wait()
-
-
-def mlp_bwd(dy, x1, gain, w_in, w_out, u, w_proj, o_flat, layer, oshape, cid):
-    du_half = (NFT, TOK, FT)
-    toks = sds(ALLTOK, BF)
-    return call(
-        mlp_bwd_body, (NFT,),
-        [spec(ALLTOK), spec(ALLTOK), spec((ONE, DM)), weight_cols(layer, FT), weight_cols(layer, FT, NFT),
-         out_weight(layer), U_SPEC, proj_spec(layer), spec((DM, TOK))],
-        [U_SPEC, spec(ALLTOK), spec((ONE, DM)), spec(oshape), spec((STATS, TOK)), ANY, ANY, ANY],
-        [sds((TWO, TOK, FF), BF), toks, sds((ONE, DM), F32), sds(oshape, BF), sds((STATS, TOK), F32),
-         sds((TOK, FF), BF), toks, toks],
-        scratch=[pltpu.VMEM(ALLTOK, F32), pltpu.VMEM(du_half, BF), DMA((NFT + TWO,)), DMA((NFT + TWO,))],
-        flops=TWO * TOK * DM * (DM + THREE * FF), nbytes=30 * MIB, name="mlp_bwd", cid=cid,
-    )(dy, x1, gain, w_in, w_in, w_out, u, w_proj, o_flat)
-
-
-def qkv_bwd_body(d_ref, cos_ref, sin_ref, w_ref, x_ref, g_ref, dmid_ref, dt_ref, dx_ref, gg_ref, dtr_ref,
-                 acc, dt_s, ssem, rsem):
-    step = pl.program_id(ZERO)
-    core, partner = core_and_partner()
-
-    def send(n):
-        return to_partner(partner, dt_s.at[n, ONE - core], dtr_ref.at[pl.ds(pl.multiple_of(n * LANE, LANE), LANE)],
-                          ssem.at[n], rsem.at[n])
-
-    @pl.when(step == ZERO)
-    def _():
-        acc[...] = jnp.zeros(acc.shape, F32)
-        meet_partner(partner)
-
-    def put(head, row, val):
-        at = row + HEAD * (head % TWO)
-        dt_s[step, head // TWO, at:at + val.shape[ZERO]] = val
-
-    @pl.when(step < ROPED)
+
+    def put(chunk, head, row, val):
+        at = LANE * chunk + row + HEAD * (head % TWO)
+        dt_s[head // TWO, step, at:at + val.shape[ZERO]] = val
+        at = RB * chunk + row + HEAD * head
+        dt_all[at:at + val.shape[ZERO]] = val
+
+    @pl.when(step < TWO)
     def _():
         cos, sin = cos_ref[...], sin_ref[...]
-        for head in range(FOUR):
-            d_head = head_rows(d_ref, head)[...].astype(F32)
-            da, db = d_head[:HALF], d_head[HALF:]
-            put(head, ZERO, (da * cos + db * sin).astype(BF))
-            put(head, HALF, (db * cos - da * sin).astype(BF))
-
-    @pl.when(step >= ROPED)
-    def _():
-        for head in range(FOUR):
-            put(head, ZERO, head_rows(d_ref, head)[...])
-
-    send(step).start()
-    dt = dt_s[step]
-    dt_ref[...] = dt
-    acc[...] += mm(w_ref[...], dt.reshape(QT, TOK))
-
-    @pl.when(step == PARTS - ONE)
+        for chunk in CHUNKS:
+            for head in range(FOUR):
+                d_head = head_rows(d_ref, chunk, head)[...].astype(F32)
+                da, db = d_head[:HALF], d_head[HALF:]
+                put(chunk, head, ZERO, (da * cos + db * sin).astype(BF))
+                put(chunk, head, HALF, (db * cos - da * sin).astype(BF))
+
+    @pl.when(step == TWO)
+    def _():
+        for chunk in CHUNKS:
+            for head in range(FOUR):
+                put(chunk, head, ZERO, head_rows(d_ref, chunk, head)[...])
+
+    for cp in copies(step):
+        cp.start()
+    acc[...] += mm(w_ref[...], dt_all[...])
+
+    @pl.when(step == TWO)
     def _():
         d_ln, gg = norm_rows_grad(x_ref[...], g_ref[...], acc[...].T.astype(BF))
         gg_ref[...] = gg
         dx_ref[...] = add_bf(dmid_ref[...], d_ln)
-        for n in range(PARTS):
-            send(n).wait()
+        for n in range(THREE):
+            for cp in copies(n):
+                cp.wait()
 
 
 def qkv_bwd(d_qkv, cos_t, sin_t, w_qkv, x, gain, d_mid, layer, dest_major, cid):
     table = spec((HALF, TOK))
-    feats = PARTS * LANE
+    half = sds((THREE * PROJ, TOK), BF)
     return call(
-        qkv_bwd_body, (PARTS,),
-        [heads_spec(dest_major), table, table, weight_cols(layer, QT), spec(ALLTOK), spec((ONE, DM)), spec(ALLTOK)],
-        [spec((TWO, LANE, TOK), ZERO, step_of, ZERO), spec(ALLTOK), spec((ONE, DM)), ANY],
-        [sds((TWO, feats, TOK), BF), sds(ALLTOK, BF), sds((ONE, DM), F32), sds((feats, TOK), BF)],
-        scratch=[pltpu.VMEM((DM, TOK), F32), pltpu.VMEM((PARTS, TWO, LANE, TOK), BF), DMA((PARTS,)), DMA((PARTS,))],
+        qkv_bwd_body, (THREE,),
+        [heads_spec(dest_major), table, table, weight_cols(layer, DM), spec(ALLTOK), spec((ONE, DM)), spec(ALLTOK)],
+        [spec(ALLTOK), spec((ONE, DM)), ANY, ANY],
+        [sds(ALLTOK, BF), sds((ONE, DM), F32), half, half],
+        scratch=[pltpu.VMEM((DM, TOK), F32), pltpu.VMEM((TWO, THREE, PROJ, TOK), BF), pltpu.VMEM((DM, TOK), BF),
+                 DMA((THREE,)), DMA((THREE,)), DMA((THREE,))],
         flops=TWO * TOK * DM * THREE * DM, nbytes=10 * MIB, name="qkv_bwd", cid=cid,
     )(d_qkv, cos_t, sin_t, w_qkv, x, gain, d_mid)
 
 
 DOWN = FF // TWO
 UP = FF
-PROJ = DM // TWO
-QKV = PARTS * LANE
+QKV = THREE * PROJ
 LAYER_ROWS = DOWN + UP + PROJ + QKV
 ALLROWS = TWO * LAYER_ROWS
-NDOWN = DOWN // RB
-NK = DM // RB
-
-
-def up_step(s):
-    return jnp.maximum(s - NDOWN, ZERO)
-
-
-def down_step(s):
-    return jnp.minimum(s, NDOWN - ONE)
-
-
-def grad_mlp_body(core_s, g_ref, ma, mb, dya, dyb, ha, hb, dua, dub, out_ref):
-    step = pl.program_id(ZERO)
-
-    @pl.when(step < NDOWN)
-    def _():
-        out_ref[...] = mm_tn(ma[...], dya[...]) + mm_tn(mb[...], dyb[...])
-
-    @pl.when(step >= NDOWN)
-    def _():
-        out_ref[...] = mm_tn(ha[...], dua[...]) + mm_tn(hb[...], dub[...])
-
-
-def grad_call(body, core, grads, steps, in_specs, args, rows, first):
+NDOWN = DOWN // DM
+GRAD_REFS = 9
+
+
+def grad_call(body, grads, steps, in_specs, args, rows, first, scratch=()):
     shared = [] if grads is None else [grads]
     return call(
         body, (steps,), [ANY] * len(shared) + in_specs,
-        spec((rows, DM), lambda s, c: first + s, ZERO), sds((ALLROWS, DM), F32),
-        prefetch=ONE, flops=FOUR * steps * rows * TOK * DM, nbytes=20 * MIB, name=body.__name__,
-        alias={ONE: ZERO} if shared else None,
-    )(core, *shared, *args)
-
-
-def grad_mlp_body(core_s, *refs):
-    ma, mb, dya, dyb, ha, hb, dua, dub, out_ref = refs[-PARTS:]
+        spec((rows, DM), lambda s: first + s, ZERO), sds((ALLROWS, DM), F32), scratch=scratch,
+        flops=FOUR * steps * rows * TOK * DM, nbytes=20 * MIB, name=body.__name__,
+        alias={ZERO: ZERO} if shared else None,
+    )(*shared, *args)
+
+
+def grad_mlp_body(*refs):
+    ma, mb, dya, dyb, ha, hb, dua, dub, out_ref, h_t = refs[-GRAD_REFS - ONE:]
     step = pl.program_id(ZERO)
 
     @pl.when(step < NDOWN)
     def _():
         out_ref[...] = mm_tn(ma[...], dya[...]) + mm_tn(mb[...], dyb[...])
 
+    @pl.when(step == NDOWN)
+    def _():
+        h_t[ZERO] = ha[...].T
+        h_t[ONE] = hb[...].T
+
     @pl.when(step >= NDOWN)
     def _():
-        out_ref[...] = mm_tn(ha[...], dua[...]) + mm_tn(hb[...], dub[...])
-
-
-def grad_mlp(core, grads, m, m_r, dy, dy_r, h, h_r, du, du_r, first_row):
-    per_ft = FT // RB
+        out_ref[...] = mm(h_t[ZERO], dua[...]) + mm(h_t[ONE], dub[...])
+
+
+def grad_mlp(grads, m, m_r, dy, dy_r, h, h_r, du, du_r, first_row):
     toks = spec(ALLTOK)
-    hcol = spec((TOK, RB), ZERO, lambda s, c: up_step(s) % NK)
-    col = lambda s, *_: up_step(s) // NK
-    return grad_call(
-        grad_mlp_body, core, grads, NDOWN + UP // RB,
-        [spec((TOK, RB), ZERO, lambda s, c: NDOWN * c[ZERO] + down_step(s)),
-         spec((None, TOK, RB), lambda s, c: down_step(s) // per_ft, ZERO, lambda s, c: down_step(s) % per_ft),
-         toks, toks, hcol, hcol,
-         spec((None, TOK, DM), lambda s, c: c[ZERO], ZERO, col), spec(ALLTOK, ZERO, col)],
-        (m, m_r, dy, dy_r, h, h_r, du, du_r), RB, first_row // RB)
-
-
-def grad_att_body(core_s, *refs):
-    oa, ob, dma, dmb, ta, tb, ha, hb, out_ref = refs[-PARTS:]
+    m_col = spec(ALLTOK, ZERO, lambda s: jnp.minimum(s, NDOWN - ONE))
+    du_col = spec(ALLTOK, ZERO, lambda s: jnp.maximum(s - NDOWN, ZERO))
+    return grad_call(grad_mlp_body, grads, NDOWN + UP // DM, [m_col, m_col, toks, toks, toks, toks, du_col, du_col],
+                     (m, m_r, dy, dy_r, h, h_r, du, du_r), DM, first_row // DM, scratch=[pltpu.VMEM((TWO, DM, TOK), BF)])
+
+
+def grad_att_body(*refs):
+    oa, ob, dma, dmb, ta, tb, ha, hb, out_ref = refs[-GRAD_REFS:]
     step = pl.program_id(ZERO)
 
     @pl.when(step == ZERO)
@@ -718,19 +739,16 @@
         out_ref[...] = mm(ta[...], ha[...]) + mm(tb[...], hb[...])
 
 
-def grad_att(core, grads, of, of_r, dmid, dmid_r, dt, dt_r, h, h_r, first_row):
+def grad_att(grads, of, of_r, dmid, dmid_r, dt, dt_r, h, h_r, first_row):
     toks = spec(ALLTOK)
     blk = (PROJ, TOK)
-    qkv_step = lambda s, *_: jnp.maximum(s - ONE, ZERO)
-    return grad_call(
-        grad_att_body, core, grads, ONE + QKV // PROJ,
-        [spec(blk, lambda s, c: c[ZERO], ZERO), spec(blk), toks, toks,
-         spec((None,) + blk, lambda s, c: c[ZERO], qkv_step, ZERO), spec(blk, qkv_step, ZERO), toks, toks],
-        (of, of_r, dmid, dmid_r, dt, dt_r, h, h_r), PROJ, (first_row + DOWN + UP) // PROJ)
+    dt_row = spec(blk, lambda s: jnp.maximum(s - ONE, ZERO), ZERO)
+    return grad_call(grad_att_body, grads, ONE + QKV // PROJ, [spec(blk), spec(blk), toks, toks, dt_row, dt_row, toks, toks],
+                     (of, of_r, dmid, dmid_r, dt, dt_r, h, h_r), PROJ, (first_row + DOWN + UP) // PROJ)
 
 
 NB, NS, CH, SB, LF = 4, 6, 128, 32, 8
-RS = PARTS
+RS = 9
 LAST = RS + RS
 
 
@@ -940,8 +958,10 @@
 
 
 def turn_body(a_ref, b_ref, out_ref):
-    out_ref[ZERO, :, :LANE] = a_ref[ZERO].T
-    out_ref[ZERO, :, LANE:] = b_ref[ZERO].T
+    for n in CHUNKS:
+        rows, col = slice(LANE * n, LANE * n + LANE), RB * n
+        out_ref[ZERO, :, col:col + LANE] = a_ref[ZERO, rows].T
+        out_ref[ZERO, :, col + LANE:col + RB] = b_ref[ZERO, rows].T
 
 
 def unpack(f):
@@ -961,10 +981,10 @@
     half, at_proj = blk(PROJ, DOWN + UP)
     g_proj = call(copy_body, (TWO, TWO), [spec(half, core_of, at_proj, ZERO)], spec(half, layer_of, core_of, ZERO),
                   sds((TWO, DM, DM), F32), nbytes=nbytes)(f)
-    lane, at_qkv = blk(LANE, DOWN + UP + PROJ)
+    part, at_qkv = blk(PROJ, DOWN + UP + PROJ)
     row = lambda l, s: at_qkv(l) + s
-    g_qkv = call(turn_body, (TWO, PARTS), [spec(lane, ZERO, row, ZERO), spec(lane, ONE, row, ZERO)],
-                 spec((ONE, DM, QT), layer_of, ZERO, lambda l, s: s), sds((TWO, DM, THREE * DM), F32), nbytes=nbytes)(f, f)
+    g_qkv = call(turn_body, (TWO, THREE), [spec(part, ZERO, row, ZERO), spec(part, ONE, row, ZERO)],
+                 spec(whole, layer_of, ZERO, core_of), sds((TWO, DM, THREE * DM), F32), nbytes=nbytes)(f, f)
     return g_qkv, g_proj, g_in, g_out
 
 
@@ -979,7 +999,7 @@
     n_sp = mesh.shape['sp']
     to_right = [(i, i + ONE) for i in range(n_sp - ONE)]
     to_left = [(i + ONE, i) for i in range(n_sp - ONE)]
-    cids = list(range(PARTS))
+    cids = list(range(RS))
 
     def halo_swap(arr):
         from_left = lax.ppermute(arr[..., TOK - LANE:], 'sp', to_right)
@@ -991,7 +1011,6 @@
 
     def device_step(x_loc, cu_loc, pos_loc, w_qkv, w_proj, w_in, w_out, ln_attn, ln_mlp, d_out):
         sp = lax.axis_index('sp')
-        core = (lax.axis_index('dp') % TWO).reshape(ONE)
         cu = cu_loc[ZERO][:, None]
 
         def bounds_of(tok):
@@ -1009,35 +1028,34 @@
                 jnp.where(inside, jnp.minimum(stop_x, tok_x + WIN + ONE) - shift, ZERO)[None, :])
         tab0, tab1 = [rope_tables(pos_loc, base) for base in BASES]
         la0, la1, lm0, lm1 = ln_attn[:ONE], ln_attn[ONE:], ln_mlp[:ONE], ln_mlp[ONE:]
-        per_head = (NHEAD, HEAD, TOK)
-
+
+        w_mlp = (w_in, w_out)
         h0, qkv0, h0r = qkv_fwd(x_loc, la0, w_qkv, ZERO, *tab0, True, cids[ONE])
         qkv0 = exchange(qkv0)
         oh0, lse0 = attn0_fwd(*tiles, qkv0, *rows)
-        x01, h02, u0, m0, x1, of0, m0r, h02r, of0r = mlp_fwd(x_loc, exchange(oh0), w_proj, lm0, w_in, w_out, ZERO, cids[TWO])
+        f0 = mlp_call(ZERO, cids[TWO], True, False, w_proj, lm0, *w_mlp, x=x_loc, o_t=exchange(oh0))
+        x1 = f0.y
         h1, qkv1, h1r = qkv_fwd(x1, la1, w_qkv, ONE, *tab1, False, cids[THREE])
         qkv1 = qkv1.reshape((THREE * NHEAD, HEAD, TOK))
         kv_halo = halo_swap(qkv1[NHEAD:])
         o1, lse1 = attn1_fwd(qkv1, *kv_halo, *near)
-        x11, h12, u1, m1, y, of1, m1r, h12r, of1r = mlp_fwd(x1, o1, w_proj, lm1, w_in, w_out, ONE, cids[FOUR])
-        du1, dmid1, ggm1, do1, del1, du1r, dy1r, dmid1r = mlp_bwd(
-            d_out, x11, lm1, w_in, w_out, u1, w_proj, of1, ONE, per_head, cids[5])
-        d_halo = halo_swap(jnp.concatenate([qkv1[:NHEAD], do1], axis=ZERO))
-        stats = jnp.concatenate([lse1.reshape(NHEAD, TOK), del1[:NHEAD]], axis=ZERO)
+        f1 = mlp_call(ONE, cids[FOUR], True, True, w_proj, lm1, *w_mlp, x=x1, o_t=o1, dy=d_out, oshape=(NHEAD, HEAD, TOK))
+        d_halo = halo_swap(jnp.concatenate([qkv1[:NHEAD], f1.d_o], axis=ZERO))
+        stats = jnp.concatenate([lse1.reshape(NHEAD, TOK), f1.delta[:NHEAD]], axis=ZERO)
         from_left, from_right = halo_swap(stats)
         lse_x, del_x = jnp.concatenate([from_left, stats, from_right], axis=ONE).reshape(TWO, NHEAD, ONE, EXT)
-        dqkv1 = attn1_bwd(qkv1, do1, *kv_halo, *d_halo, lse_x, del_x, *near)
-        dt1, dx1, gga1, dt1r = qkv_bwd(dqkv1.reshape(THREE, THREE, FOUR, HEAD, TOK), *tab1, w_qkv, x1, la1, dmid1,
+        dqkv1 = attn1_bwd(qkv1, f1.d_o, *kv_halo, *d_halo, lse_x, del_x, *near)
+        dx1, gga1, dt1, dt1r = qkv_bwd(dqkv1.reshape(THREE, THREE, FOUR, HEAD, TOK), *tab1, w_qkv, x1, la1, f1.dmid,
                                        ONE, False, cids[SIX])
-        grads = grad_mlp(core, None, m1, m1r, d_out, dy1r, h12, h12r, du1, du1r, ZERO)
-        grads = grad_att(core, grads, of1, of1r, dmid1, dmid1r, dt1, dt1r, h1, h1r, ZERO)
-        du0, dmid0, ggm0, do0, _, du0r, dy0r, dmid0r = mlp_bwd(
-            dx1, x01, lm0, w_in, w_out, u0, w_proj, of0, ZERO, oh0.shape, cids[7])
-        grads = grad_mlp(core, grads, m0, m0r, dx1, dy0r, h02, h02r, du0, du0r, LAYER_ROWS)
-        dqkv0 = exchange(attn0_bwd(*tiles, qkv0, oh0, exchange(do0), lse0, *rows))
-        dt0, dx0, gga0, dt0r = qkv_bwd(dqkv0, *tab0, w_qkv, x_loc, la0, dmid0, ZERO, True, cids[8])
-        grads = grad_att(core, grads, of0, of0r, dmid0, dmid0r, dt0, dt0r, h0, h0r, LAYER_ROWS)
-
+        grads = grad_mlp(None, f1.m_m, f1.m_r, d_out, f1.dy_r, f1.h, f1.h_r, f1.du_m, f1.du_r, ZERO)
+        grads = grad_att(grads, f1.of_m, f1.of_r, f1.dmid, f1.dmid_r, dt1, dt1r, h1, h1r, ZERO)
+        b0 = mlp_call(ZERO, cids[5], False, True, w_proj, lm0, *w_mlp, dy=dx1, x1=f0.x1, u=f0.u, oshape=oh0.shape)
+        grads = grad_mlp(grads, f0.m_m, f0.m_r, dx1, b0.dy_r, f0.h, f0.h_r, b0.du_m, b0.du_r, LAYER_ROWS)
+        dqkv0 = exchange(attn0_bwd(*tiles, qkv0, oh0, exchange(b0.d_o), lse0, *rows))
+        dx0, gga0, dt0, dt0r = qkv_bwd(dqkv0, *tab0, w_qkv, x_loc, la0, b0.dmid, ZERO, True, cids[7])
+        grads = grad_att(grads, f0.of_m, f0.of_r, b0.dmid, b0.dmid_r, dt0, dt0r, h0, h0r, LAYER_ROWS)
+
+        y, ggm0, ggm1 = f1.y, b0.gg, f1.gg
         gains = jnp.concatenate([gga0, gga1, ggm0, ggm1, jnp.zeros((FOUR, DM), F32)], axis=ZERO)
         summed, gains = ring_all_reduce(grads, gains, cids[ZERO])
         return (y, dx0) + unpack(summed) + (gains[:TWO], gains[TWO:FOUR])

time: 789 us -> 739 us (0.937)
  Pallas kernels: 676 us -> 616 us
    pallas_call x11 -> x10, Pallas kernels: 202 us -> 156 us  [the longest x3 71.5 us: mlp_call(): call(functools.partial(mlp_body, names=names, fwd=fwd, bwd=bwd), (NFT,),...]
    pallas_call x4, Pallas kernels: 58 us -> 44.2 us  [grad_call(): call(body, (steps,), [ANY] * len(shared) + in_specs, spec((rows, DM), lam...]
  transfers between devices with their start and end apart: 9 -> 9, of which waited for: 6 -> 6; matrix products, arithmetic and copies ran while one was open for 1% -> 1% of each run, Pallas kernels for 6% -> 5%
where the time goes in v2:
time: 739 us; the launch traced here: 732 us
  Pallas kernels  616 us (83%)
  waiting for transfers between devices  48.3 us (7%)
  starting transfers between devices  27.9 us (4%)
  local copies, waits for them, and re-layouts  16.8 us (2%)
  blocking collectives  16.1 us (2%)
    pallas_call x1, Pallas kernels, ring_all_reduce(): pl.pallas_call(ring_body, in_specs=[ANY, vmem], out_specs=[ANY, vmem], ou...  299 us
    pallas_call x3, Pallas kernels, mlp_call(): call(functools.partial(mlp_body, names=names, fwd=fwd, bwd=bwd), (NFT,),...  71.5 us
    pallas_call x4, Pallas kernels, grad_call(): call(body, (steps,), [ANY] * len(shared) + in_specs, spec((rows, DM), lam...  44.2 us
    all_to_all x3, waiting for transfers between devices, exchange(): return lax.all_to_all(arr, 'sp', ZERO, ZERO, tiled=True)  39.7 us
    pallas_call x1, Pallas kernels, attn0_bwd(): call(attn0_bwd_body, (QTILES,), [Q_SPEC, kv_spec(ONE), kv_spec(TWO), O_SP...  33.8 us
    pallas_call x1, Pallas kernels, attn0_fwd(): call(attn0_fwd_body, (QTILES,), [Q_SPEC, kv_spec(ONE), kv_spec(TWO), ROW_...  32.2 us
    pallas_call x1, Pallas kernels, unpack(): call(copy_body, (TWO, TWO, FOUR), [spec(whole, core_of, lambda l, c, j: a...  29.7 us
    pallas_call x1, Pallas kernels, attn1_bwd(): call(attn1_bwd_body, (HSTEPS,), [own_head(ZERO), own_head(ONE), own_head(...  21 us
  transfers between devices with their start and end apart: 9, of which 6 were waited for; matrix products, arithmetic and copies ran while one was open for 1% of the time, Pallas kernels for 5%

profile of v2, /device:TPU:1, one launch (start us, length us, event | category | flops | bytes accessed | tf_op | source)
XLA Modules:
  0.0 732.0 jit_solution(14062704452806498749)
XLA Ops:
  3.9 7.9 %qkv_fwd.2 = (bf16[512,768]{1,0:T(8,128)(2,1)}, bf16[4,3,3,64,512]{4,3,2,1,0:T(8,128)(2,1)}, bf16[512,768]{1,0:T(8,128)(2,1)}) custom-call(bf16[512,768]{1,0:T(8,128)(2,1)} %x_ref.3, f32[1,768]{1,0:T(1,128)} %get-tuple-element.125.g_ref, bf16[2,768,2304]{2,1,0:T(8,128)(2,1)} %w_ref.7, f32[32,512]{1,0:T(8,128)} %get-tuple-element.132.cos_ref, ...), custom_call_target="tpu_custom_call" | custom-call | flops 1811939328 | bytes 8388608 | tf_op jit(solution)/shard_map/qkv_fwd/pallas_call | solution.py:182
  11.8 4.2 all-to-all-start
  16.9 27.8 %all-to-all-done.q_ref.k_ref.v_ref = bf16[4,3,3,64,512]{4,3,2,1,0:T(8,128)(2,1)S(1)} async-done(((bf16[4,3,3,64,512]{4,3,2,1,0:T(8,128)(2,1)}), bf16[4,3,3,64,512]{4,3,2,1,0:T(8,128)(2,1)S(1)}, u32[]{:S(2)}, u32[]{:S(2)}) %all-to-all-start) | async-done | bytes 2359328 | tf_op jit(solution)/shard_map/all_to_all | solution.py:1010
  46.1 32.2 %attn0_fwd.1 = (bf16[4,3,64,512]{3,2,1,0:T(8,128)(2,1)}, f32[8,2048]{1,0:T(8,128)}) custom-call(s32[8]{0:T(128)} %get-tuple-element.137.lo_s, s32[8]{0:T(128)} %get-tuple-element.136.hi_s, bf16[4,3,3,64,512]{4,3,2,1,0:T(8,128)(2,1)} %copy-done.4, bf16[4,3,3,64,512]{4,3,2,1,0:T(8,128)(2,1)} %copy-done.4, bf16[4,3,3,64,512]{4,3,2,1,0:T(8,128)(2,1)} %copy-done.4, ...), custom_call_target="tpu_custom_call" | custom-call | flops 3221225472 | bytes 6291456 | tf_op jit(solution)/shard_map/attn0_fwd/pallas_call | solution.py:251
  78.4 3.5 all-to-all-start.1
  82.5 11.9 %all-to-all-done.1.refs_6_ = bf16[4,3,64,512]{3,2,1,0:T(8,128)(2,1)S(1)} async-done(((bf16[4,3,64,512]{3,2,1,0:T(8,128)(2,1)}), bf16[4,3,64,512]{3,2,1,0:T(8,128)(2,1)S(1)}, u32[]{:S(2)}, u32[]{:S(2)}) %all-to-all-start.1) | async-done | bytes 786464 | tf_op jit(solution)/shard_map/all_to_all | solution.py:1010
  95.2 19.4 %mlp_fwd.1 = (bf16[512,768]{1,0:T(8,128)(2,1)}, bf16[512,768]{1,0:T(8,128)(2,1)}, bf16[512,768]{1,0:T(8,128)(2,1)}, bf16[384,512]{1,0:T(8,128)(2,1)}, bf16[384,5...) custom-call(bf16[2,768,768]{2,1,0:T(8,128)(2,1)} %refs_0_.5, ...), custom_call_target="tpu_custom_call" | custom-call | flops 7851737088 | bytes 27262976 | tf_op jit(solution)/shard_map/mlp_fwd/pallas_call | solution.py:608
  114.6 6.9 qkv_fwd.3
  121.5 1.5 slice.65
  124.6 4.2 collective-permute-start
  130.7 4.8 collective-permute-done.1.kr_ref.vr_ref
  137.1 18.0 %attn1_fwd.1 = (bf16[12,64,512]{2,1,0:T(8,128)(2,1)}, f32[12,1,512]{2,1,0:T(1,128)}) custom-call(bf16[36,64,512]{2,1,0:T(8,128)(2,1)} %bitcast.13, bf16[36,64,512]{2,1,0:T(8,128)(2,1)} %bitcast.14, bf16[36,64,512]{2,1,0:T(8,128)(2,1)} %bitcast.15, bf16[24,64,128]{2,1,0:T(8,128)(2,1)} %copy-done.2, bf16[24,64,128]{2,1,0:T(8,128)(2,1)} %copy-done.2, ...), custom_call_target="tpu_custom_call" | custom-call | flops 603979776 | bytes 4194304 | tf_op jit(solution)/shard_map/attn1_fwd/pallas_call | solution.py:376
  155.9 31.8 %mlp_fwdbwd.1 = (bf16[512,768]{1,0:T(8,128)(2,1)}, bf16[512,768]{1,0:T(8,128)(2,1)}, bf16[512,768]{1,0:T(8,128)(2,1)}, bf16[384,512]{1,0:T(8,128)(2,1)}, bf16[38...) custom-call(bf16[2,768,768]{2,1,0:T(8,128)(2,1)} %refs_0_.5, ...), custom_call_target="tpu_custom_call" | custom-call | flops 15703474176 | bytes 27262976 | tf_op jit(solution)/shard_map/mlp_fwdbwd/pallas_call | solution.py:608
  190.2 4.8 collective-permute-start.2
  195.7 3.3 collective-permute-start.4
  200.6 2.8 collective-permute-done.4
  207.1 21.0 %attn1_bwd.1 = bf16[3,12,64,512]{3,2,1,0:T(8,128)(2,1)} custom-call(bf16[36,64,512]{2,1,0:T(8,128)(2,1)} %bitcast.16, bf16[36,64,512]{2,1,0:T(8,128)(2,1)} %bitcast.17, bf16[36,64,512]{2,1,0:T(8,128)(2,1)} %bitcast.18, bf16[12,64,512]{2,1,0:T(8,128)(2,1)} %get-tuple-element.65.do_ref, bf16[24,64,128]{2,1,0:T(8,128)(2,1)} %copy-done.2, ...), custom_call_target="tpu_custom_call" | custom-call | flops 1509949440 | bytes 8388608 | tf_op jit(solution)/shard_map/attn1_bwd/pallas_call | solution.py:422
  228.1 10.4 %qkv_bwd.2 = (bf16[512,768]{1,0:T(8,128)(2,1)}, f32[1,768]{1,0:T(1,128)}, bf16[1152,512]{1,0:T(8,128)(2,1)}, bf16[1152,512]{1,0:T(8,128)(2,1)}) custom-call(bf16[3,3,4,64,512]{4,3,2,1,0:T(8,128)(2,1)} %bitcast.19, f32[32,512]{1,0:T(8,128)} %get-tuple-element.129.cos_ref, f32[32,512]{1,0:T(8,128)} %get-tuple-element.128.sin_ref, bf16[2,768,2304]{2,1,0:T(8,128)(2,1)} %w_ref.7, ...), custom_call_target="tpu_custom_call" | custom-call | flops 1811939328 | bytes 10485760 | tf_op jit(solution)/shard_map/qkv_bwd/pallas_call | solution.py:673
  238.5 20.3 %mlp_bwd.1 = (bf16[512,768]{1,0:T(8,128)(2,1)}, f32[1,768]{1,0:T(1,128)}, bf16[4,3,64,512]{3,2,1,0:T(8,128)(2,1)}, bf16[512,768]{1,0:T(8,128)(2,1)}, bf16[512,76...) custom-call(bf16[2,768,768]{2,1,0:T(8,128)(2,1)} %refs_0_.5, ...), custom_call_target="tpu_custom_call" | custom-call | flops 7851737088 | bytes 27262976 | tf_op jit(solution)/shard_map/mlp_bwd/pallas_call | solution.py:608
  258.9 16.1 %all_to_all.20.do_ref = bf16[4,3,64,512]{3,2,1,0:T(8,128)(2,1)} all-to-all(bf16[4,3,64,512]{3,2,1,0:T(8,128)(2,1)} %get-tuple-element.72), channel_id=1, replica_groups=mesh['sp'=4,'dp'=32] {'sp'}, dimensions={0} | all-to-all | bytes 1572864 | tf_op jit(solution)/shard_map/all_to_all | solution.py:1010
  275.0 33.8 %attn0_bwd.1 = bf16[4,3,3,64,512]{4,3,2,1,0:T(8,128)(2,1)} custom-call(s32[8]{0:T(128)} %get-tuple-element.137.lo_s, s32[8]{0:T(128)} %get-tuple-element.136.hi_s, bf16[4,3,3,64,512]{4,3,2,1,0:T(8,128)(2,1)} %copy-done.4, bf16[4,3,3,64,512]{4,3,2,1,0:T(8,128)(2,1)} %copy-done.4, bf16[4,3,3,64,512]{4,3,2,1,0:T(8,128)(2,1)} %copy-done.4, ...), custom_call_target="tpu_custom_call" | custom-call | flops 8053063680 | bytes 12582912 | tf_op jit(solution)/shard_map/attn0_bwd/pallas_call | solution.py:308
  308.8 3.9 all-to-all-start.3
  312.7 14.7 %grad_mlp_body.2.refs_0_ = f32[12288,768]{1,0:T(8,128)} custom-call(bf16[512,1536]{1,0:T(8,128)(2,1)} %get-tuple-element.76.refs_0_, bf16[512,1536]{1,0:T(8,128)(2,1)} %get-tuple-element.77.refs_1_, bf16[512,768]{1,0:T(8,128)(2,1)} %refs_2_.7, bf16[512,768]{1,0:T(8,128)(2,1)} %get-tuple-element.78.refs_3_, bf16[512,768]{1,0:T(8,128)(2,1)} %get-tuple-element.79.refs_4_, ...), custom_call_target="tpu_custom_call" | custom-call | flops 7247757312 | bytes 20971520 | tf_op jit(solution)/shard_map/grad_mlp_body/pallas_call | solution.py:695
  327.4 7.3 %grad_att_body.2.refs_0_ = f32[12288,768]{1,0:T(8,128)} custom-call(f32[12288,768]{1,0:T(8,128)} %grad_mlp_body.2.refs_0_, bf16[384,512]{1,0:T(8,128)(2,1)} %get-tuple-element.83.refs_1_, bf16[384,512]{1,0:T(8,128)(2,1)} %get-tuple-element.84.refs_2_, bf16[512,768]{1,0:T(8,128)(2,1)} %get-tuple-element.68.dmid_ref.refs_3_, ...), custom_call_target="tpu_custom_call", output_to_operand_aliasing={{}: (0, {})} | custom-call | flops 2415919104 | bytes 20971520 | tf_op jit(solution)/shard_map/grad_att_body/pallas_call | solution.py:695
  334.8 14.8 %grad_mlp_body.3.refs_0_ = f32[12288,768]{1,0:T(8,128)} custom-call(f32[12288,768]{1,0:T(8,128)} %grad_att_body.2.refs_0_, bf16[512,1536]{1,0:T(8,128)(2,1)} %get-tuple-element.90.refs_1_, bf16[512,1536]{1,0:T(8,128)(2,1)} %get-tuple-element.91.refs_2_, bf16[512,768]{1,0:T(8,128)(2,1)} %get-tuple-element.69.refs_5_.refs_3_, ...), custom_call_target="tpu_custom_call", output_to_operand_aliasing={{}: (0, {})} | custom-call | flops 7247757312 | bytes 20971520 | tf_op jit(solution)/shard_map/grad_mlp_body/pallas_call | solution.py:695
  351.0 8.1 %qkv_bwd.3 = (bf16[512,768]{1,0:T(8,128)(2,1)}, f32[1,768]{1,0:T(1,128)}, bf16[1152,512]{1,0:T(8,128)(2,1)}, bf16[1152,512]{1,0:T(8,128)(2,1)}) custom-call(bf16[4,3,3,64,512]{4,3,2,1,0:T(8,128)(2,1)} %copy-done, f32[32,512]{1,0:T(8,128)} %get-tuple-element.132.cos_ref, f32[32,512]{1,0:T(8,128)} %get-tuple-element.133.sin_ref, bf16[2,768,2304]{2,1,0:T(8,128)(2,1)} %w_ref.7, ...), custom_call_target="tpu_custom_call" | custom-call | flops 1811939328 | bytes 10485760 | tf_op jit(solution)/shard_map/qkv_bwd/pallas_call | solution.py:673
  360.5 7.3 %grad_att_body.3.g_ref = f32[12288,768]{1,0:T(8,128)} custom-call(f32[12288,768]{1,0:T(8,128)} %grad_mlp_body.3.refs_0_, bf16[384,512]{1,0:T(8,128)(2,1)} %get-tuple-element.97.refs_1_, bf16[384,512]{1,0:T(8,128)(2,1)} %get-tuple-element.98.refs_2_, bf16[512,768]{1,0:T(8,128)(2,1)} %get-tuple-element.74.dmid_ref.refs_3_, ...), custom_call_target="tpu_custom_call", output_to_operand_aliasing={{}: (0, {})} | custom-call | flops 2415919104 | bytes 20971520 | tf_op jit(solution)/shard_map/grad_att_body/pallas_call | solution.py:695
  367.8 299.1 %ring_all_reduce.1 = (f32[2,12288,768]{2,1,0:T(8,128)}, f32[8,768]{1,0:T(8,128)}) custom-call(f32[12288,768]{1,0:T(8,128)} %grad_att_body.3.g_ref, f32[8,768]{1,0:T(8,128)} %concatenate.15.ln_ref), custom_call_target="tpu_custom_call" | custom-call | tf_op jit(solution)/shard_map/ring_all_reduce/pallas_call | solution.py:939
  666.9 5.1 shard_map.162
  672.0 12.5 %shard_map.161 = f32[2,768,2304]{2,1,0:T(8,128)} custom-call(f32[2,12288,768]{2,1,0:T(8,128)} %get-tuple-element.108.a_ref.b_ref.in_ref, f32[2,12288,768]{2,1,0:T(8,128)} %get-tuple-element.108.a_ref.b_ref.in_ref), custom_call_target="tpu_custom_call" | custom-call | bytes 104857600 | tf_op jit(solution)/shard_map/pallas_call | solution.py:986
  684.5 15.0 %shard_map.164 = f32[2,3072,768]{2,1,0:T(8,128)} custom-call(f32[2,12288,768]{2,1,0:T(8,128)} %get-tuple-element.108.a_ref.b_ref.in_ref), custom_call_target="tpu_custom_call" | custom-call | bytes 104857600 | tf_op jit(solution)/shard_map/pallas_call | solution.py:975
  699.5 29.7 %shard_map.163 = f32[2,768,6144]{2,1,0:T(8,128)} custom-call(f32[2,12288,768]{2,1,0:T(8,128)} %get-tuple-element.108.a_ref.b_ref.in_ref), custom_call_target="tpu_custom_call" | custom-call | bytes 104857600 | tf_op jit(solution)/shard_map/pallas_call | solution.py:978
  (68 shorter events, 26.3 us)
Async XLA Ops:
  11.8 4.2 copy-start.16
  11.8 32.9 %all-to-all-start = ((bf16[4,3,3,64,512]{4,3,2,1,0:T(8,128)(2,1)}), bf16[4,3,3,64,512]{4,3,2,1,0:T(8,128)(2,1)S(1)}, u32[]{:S(2)}, u32[]{:S(2)}) async-start(bf16[4,3,3,64,512]{4,3,2,1,0:T(8,128)(2,1)} %get-tuple-element.59), calls=%async_computation | async-start | bytes 4718592 | tf_op jit(solution)/shard_map/all_to_all | solution.py:1010
  16.1 28.6 %copy-start.9 = (s32[2048]{0:T(1024)}, s32[2048]{0:T(1024)S(1)}, u32[]{:S(2)}) copy-start(s32[2048]{0:T(1024)S(1)} %get-tuple-element.112) | copy-start | bytes 24580
  16.1 28.6 %copy-start.10 = (s32[2048]{0:T(1024)}, s32[2048]{0:T(1024)S(1)}, u32[]{:S(2)}) copy-start(s32[2048]{0:T(1024)S(1)} %get-tuple-element.113) | copy-start | bytes 24580
  44.7 1.4 copy-start.4
  46.1 35.8 %copy-start.12 = (f32[2,768]{1,0:T(2,128)S(1)}, f32[2,768]{1,0:T(2,128)}, u32[]{:S(2)}) copy-start(f32[2,768]{1,0:T(2,128)} %param.18) | copy-start | bytes 18436
  78.4 16.0 %all-to-all-start.1 = ((bf16[4,3,64,512]{3,2,1,0:T(8,128)(2,1)}), bf16[4,3,64,512]{3,2,1,0:T(8,128)(2,1)S(1)}, u32[]{:S(2)}, u32[]{:S(2)}) async-start(bf16[4,3,64,512]{3,2,1,0:T(8,128)(2,1)} %get-tuple-element.60.o_ref), calls=%async_computation.1 | async-start | bytes 1572864 | tf_op jit(solution)/shard_map/all_to_all | solution.py:1010
  94.3 0.9 copy-start.3
  123.3 12.3 %collective-permute-start.1 = (bf16[24,64,128]{2,1,0:T(8,128)(2,1)S(1)}, bf16[24,64,128]{2,1,0:T(8,128)(2,1)S(1)}, u32[]{:S(2)}, u32[]{:S(2)}) collective-permute-start(bf16[24,64,128]{2,1,0:T(8,128)(2,1)S(1)} %get-tuple-element.116), channel_id=1, source_target_pairs={{32,0},{64,32},{96,64},{33,1},{65,33},{97,65},{34,2},{66,34},{98,6... | collective-permute-start | bytes 1179656 | tf_op jit(solution)/shard_map/ppermute | solution.py:1006
  124.6 11.8 %collective-permute-start = (bf16[24,64,128]{2,1,0:T(8,128)(2,1)S(1)}, bf16[24,64,128]{2,1,0:T(8,128)(2,1)S(1)}, u32[]{:S(2)}, u32[]{:S(2)}) collective-permute-start(bf16[24,64,128]{2,1,0:T(8,128)(2,1)S(1)} %get-tuple-element.117), channel_id=1, source_target_pairs={{0,32},{32,64},{64,96},{1,33},{33,65},{65,97},{2,34},{34,66},{66,9... | collective-permute-start | bytes 1179656 | tf_op jit(solution)/shard_map/ppermute | solution.py:1005
  135.5 0.9 copy-start.1
  136.4 0.7 copy-start.2
  188.9 16.7 %collective-permute-start.3 = (bf16[24,64,128]{2,1,0:T(8,128)(2,1)S(1)}, bf16[24,64,128]{2,1,0:T(8,128)(2,1)S(1)}, u32[]{:S(2)}, u32[]{:S(2)}) collective-permute-start(bf16[24,64,128]{2,1,0:T(8,128)(2,1)S(1)} %get-tuple-element.114), channel_id=1, source_target_pairs={{32,0},{64,32},{96,64},{33,1},{65,33},{97,65},{34,2},{66,34},{98,6... | collective-permute-start | bytes 1179656 | tf_op jit(solution)/shard_map/ppermute | solution.py:1006
  190.2 15.4 %collective-permute-start.2 = (bf16[24,64,128]{2,1,0:T(8,128)(2,1)S(1)}, bf16[24,64,128]{2,1,0:T(8,128)(2,1)S(1)}, u32[]{:S(2)}, u32[]{:S(2)}) collective-permute-start(bf16[24,64,128]{2,1,0:T(8,128)(2,1)S(1)} %get-tuple-element.115), channel_id=1, source_target_pairs={{0,32},{32,64},{64,96},{1,33},{33,65},{65,97},{2,34},{34,66},{66,9... | collective-permute-start | bytes 1179656 | tf_op jit(solution)/shard_map/ppermute | solution.py:1005
  195.7 7.6 %collective-permute-start.4 = (f32[24,128]{1,0:T(8,128)S(1)}, f32[24,128]{1,0:T(8,128)S(1)}, u32[]{:S(2)}, u32[]{:S(2)}) collective-permute-start(f32[24,128]{1,0:T(8,128)S(1)} %get-tuple-element.120), channel_id=1, source_target_pairs={{0,32},{32,64},{64,96},{1,33},{33,65},{65,97},{2,34},{34,66},{66,9... | collective-permute-start | bytes 36872 | tf_op jit(solution)/shard_map/ppermute | solution.py:1005
  199.0 4.4 collective-permute-start.5
  205.6 0.8 copy-start.5
  206.3 0.7 copy-start.6
  308.8 40.8 %all-to-all-start.3 = ((bf16[4,3,3,64,512]{4,3,2,1,0:T(8,128)(2,1)}), bf16[4,3,3,64,512]{4,3,2,1,0:T(8,128)(2,1)S(1)}, u32[]{:S(2)}, u32[]{:S(2)}) async-start(bf16[4,3,3,64,512]{4,3,2,1,0:T(8,128)(2,1)} %attn0_bwd.1), calls=%async_computation.3 | async-start | bytes 4718592 | tf_op jit(solution)/shard_map/all_to_all | solution.py:1010
  349.6 1.4 copy-start
  351.0 8.1 %copy-start.13 = (f32[1,768]{1,0:T(1,128)S(1)}, f32[1,768]{1,0:T(1,128)}, u32[]{:S(2)}) copy-start(f32[1,768]{1,0:T(1,128)} %get-tuple-element.107) | copy-start | bytes 9220
  351.0 8.1 %copy-start.14 = (f32[1,768]{1,0:T(1,128)S(1)}, f32[1,768]{1,0:T(1,128)}, u32[]{:S(2)}) copy-start(f32[1,768]{1,0:T(1,128)} %get-tuple-element.105) | copy-start | bytes 9220
  351.0 8.1 %copy-start.15 = (f32[1,768]{1,0:T(1,128)S(1)}, f32[1,768]{1,0:T(1,128)}, u32[]{:S(2)}) copy-start(f32[1,768]{1,0:T(1,128)} %get-tuple-element.106) | copy-start | bytes 9220
  699.5 29.7 %copy-start.11 = (f32[8,768]{1,0:T(8,128)S(1)}, f32[8,768]{1,0:T(8,128)}, u32[]{:S(2)}) copy-start(f32[8,768]{1,0:T(8,128)} %get-tuple-element.109) | copy-start | bytes 73732
  699.5 30.3 %copy-start.7 = (bf16[512,768]{1,0:T(8,128)(2,1)S(1)}, bf16[512,768]{1,0:T(8,128)(2,1)}, u32[]{:S(2)}) copy-start(bf16[512,768]{1,0:T(8,128)(2,1)} %get-tuple-element.148) | copy-start | bytes 2359300
  699.5 31.2 %copy-start.8 = (bf16[512,768]{1,0:T(8,128)(2,1)S(1)}, bf16[512,768]{1,0:T(8,128)(2,1)}, u32[]{:S(2)}) copy-start(bf16[512,768]{1,0:T(8,128)(2,1)} %get-tuple-element.149) | copy-start | bytes 2359300
